TPU v7x, 8 devices: a whole 2x2x1 slice. The times are simulated.
8 devices in a mesh: data: 8 (over z, y, x, core).
Axes of the slice: x: 2, y: 2, z: 1, core: 2. Of those that a mesh axis runs over, the one named last changes fastest.
Arguments:
- z_one: bfloat16 [512, 256], P('data')
- z_two: bfloat16 [512, 256], P('data')
- z_small: bfloat16 [10, 512, 256], P(None, 'data')
- protos: bfloat16 [8192, 256], replicated
- live_mask: int32 [512], P('data')
Outputs:
- output 1: float32 [512, 8192], P('data')
- output 2: float32 [512, 8192], P('data')
- output 3: float32 [], replicated
- output 4: float32 [512, 256], P('data')
- output 5: float32 [512, 256], P('data')
- output 6: float32 [10, 512, 256], P(None, 'data')
- output 7: float32 [8192, 256], replicated
All inputs are finite; a program needn't handle non-finite values.
Results may differ from a plain program's by a relative error of at most 0.001.
Values are sent between devices in bfloat16 or wider.
A program may use at most 1 GiB of HBM per device.

v0:
```python
import jax
import jax.numpy as jnp
from jax import lax
from jax.sharding import PartitionSpec as P

EPS = 0.05
TAU = 0.1
ITERS = 3


def value_a14(scores, live_col, live_total, num_protos):
    weights = live_col * jnp.exp(scores / EPS)
    for step_idx in range(ITERS):
        col_sum = lax.psum(jnp.sum(weights, axis=0), "data")
        weights = weights / (num_protos * col_sum)
        row_sum = jnp.sum(weights, axis=1, keepdims=True)
        row_safe = jnp.where(live_col > 0, row_sum, 1.0)
        weights = weights * (live_col / (live_total * row_safe))
    return live_total * weights


def loss_and_grads(z_one, z_two, z_small, protos, scores_one, scores_two, q_one, q_two, live_col, live_total):
    pair_count = 2 + 2 * z_small.shape[0]
    grad_scale = 1.0 / (TAU * live_total * pair_count)
    scores_small = jnp.einsum("jnd,kd->jnk", z_small, protos, preferred_element_type=jnp.float32)
    logp_one = jax.nn.log_softmax(scores_one / TAU, axis=-1)
    logp_two = jax.nn.log_softmax(scores_two / TAU, axis=-1)
    logp_small = jax.nn.log_softmax(scores_small / TAU, axis=-1)
    q_sum = q_one + q_two
    cross_sum = jnp.sum(q_two * logp_one) + jnp.sum(q_one * logp_two) + jnp.sum(q_sum[None] * logp_small)
    loss_total = -lax.psum(cross_sum, "data") / (live_total * pair_count)
    grad_one = ((live_col * jnp.exp(logp_one) - q_two) * grad_scale).astype(jnp.bfloat16)
    grad_two = ((live_col * jnp.exp(logp_two) - q_one) * grad_scale).astype(jnp.bfloat16)
    grad_small = ((2.0 * live_col[None] * jnp.exp(logp_small) - q_sum[None]) * grad_scale).astype(jnp.bfloat16)
    dz_one = jnp.einsum("nk,kd->nd", grad_one, protos, preferred_element_type=jnp.float32)
    dz_two = jnp.einsum("nk,kd->nd", grad_two, protos, preferred_element_type=jnp.float32)
    dz_small = jnp.einsum("jnk,kd->jnd", grad_small, protos, preferred_element_type=jnp.float32)
    dc_part = (jnp.einsum("nk,nd->kd", grad_one, z_one, preferred_element_type=jnp.float32)
               + jnp.einsum("nk,nd->kd", grad_two, z_two, preferred_element_type=jnp.float32)
               + jnp.einsum("jnk,jnd->kd", grad_small, z_small, preferred_element_type=jnp.float32))
    d_protos = lax.psum(dc_part, "data")
    return loss_total, dz_one, dz_two, dz_small, d_protos


def local_step(z_one, z_two, z_small, protos, live_mask):
    live_f = live_mask.astype(jnp.float32)
    live_col = live_f[:, None]
    live_total = lax.psum(jnp.sum(live_f), "data")
    num_protos = protos.shape[0]
    scores_one = jnp.einsum("nd,kd->nk", z_one, protos, preferred_element_type=jnp.float32)
    q_one = value_a14(scores_one, live_col, live_total, num_protos)
    scores_two = jnp.einsum("nd,kd->nk", z_two, protos, preferred_element_type=jnp.float32)
    q_two = value_a14(scores_two, live_col, live_total, num_protos)
    loss_total, dz_one, dz_two, dz_small, d_protos = loss_and_grads(z_one, z_two, z_small, protos, scores_one, scores_two, q_one, q_two, live_col, live_total)
    return q_one, q_two, loss_total, dz_one, dz_two, dz_small, d_protos


def solution(mesh):
    row_spec = P("data", None)
    crop_spec = P(None, "data", None)
    return jax.shard_map(local_step, mesh=mesh,
                         in_specs=(row_spec, row_spec, crop_spec, P(None, None), P("data")),
                         out_specs=(row_spec, row_spec, P(), row_spec, row_spec, crop_spec, P(None, None)),
                         check_vma=False)
```

profile of v0, /device:TPU:0, one launch (start us, length us, event | category | flops | bytes accessed | tf_op | source)
XLA Modules:
  0.0 388.7 jit_solution(10291903544732350988)
XLA Ops:
  7.2 0.0 copy-start
  7.2 0.0 all-reduce.3.cloned.1.call-start
  7.2 0.7 convert_element_type.12
  7.9 1.3 broadcast_multiply_fusion.6
  9.2 3.8 multiply_reduce_fusion.4
  13.0 0.0 copy-start.5
  13.1 0.0 copy-start.16
  13.1 0.5 exponential_reduce_fusion.1
  13.6 0.2 copy-done.16
  13.8 1.5 multiply_reduce_fusion.5
  15.3 0.9 exponential_reduce_fusion.2
  16.2 25.6 %all-reduce = (f32[8192]{0:T(1024)S(1)}, f32[]{:T(128)}) all-reduce(f32[8192]{0:T(1024)S(1)} %get-tuple-element.11, f32[]{:T(128)} %get-tuple-element.31), channel_id=1, replica_groups=mesh['data'=8] {'data'}, use_global_device_ids=true, to_apply=%region_3.0 | all-reduce | flops 8193 | bytes 65544 | tf_op jit(solution)/shard_map/psum | solution.py:14
  41.8 1.9 fusion.25
  44.3 0.7 multiply_divide_fusion.9
  45.0 1.9 multiply_reduce_fusion.9
  46.8 23.2 %psum.65 = f32[8192]{0:T(1024)S(1)} all-reduce(f32[8192]{0:T(1024)S(1)} %multiply_reduce_fusion.9), channel_id=1, replica_groups=mesh['data'=8] {'data'}, use_global_device_ids=true, to_apply=%region_6.7 | all-reduce | flops 8192 | bytes 65536 | tf_op jit(solution)/shard_map/psum | solution.py:14
  70.0 2.0 fusion.24
  72.0 0.0 copy-start.7
  72.0 0.7 multiply_divide_fusion.8
  72.7 0.7 copy-done.7
  73.3 0.3 multiply_reduce_fusion.8
  73.6 24.1 %psum.66 = f32[8192]{0:T(1024)S(1)} all-reduce(f32[8192]{0:T(1024)S(1)} %multiply_reduce_fusion.8), channel_id=1, replica_groups=mesh['data'=8] {'data'}, use_global_device_ids=true, to_apply=%region_9.10 | all-reduce | flops 8192 | bytes 65536 | tf_op jit(solution)/shard_map/psum | solution.py:14
  97.8 2.0 fusion.18
  99.7 0.7 multiply_divide_fusion.7
  100.4 0.0 copy-start.6
  100.5 5.0 %multiply_convert_fusion.1 = (bf16[64,8192]{1,0:T(8,128)(2,1)}, f32[64,8192]{1,0:T(8,128)S(1)}) fusion(f32[64,8192]{1,0:T(8,128)} %copy-done.5, f32[64]{0:T(128)S(1)} %log.20, f32[64]{0:T(128)S(1)} %get-tuple-element.32, f32[]{:T(128)S(6)} %div.121, f32[64]{0:T(128)S(1)} %convert_element_type.12, f32[64]{0:T(128)S(1)} %multiply_divide_fusion.7, ...), kind=kLoop, calls=%fused_computation.20 | loop fusion | flops 5767168 | bytes 7374088 | tf_op jit(solution)/shard_map/convert_element_type | solution.py:33
  105.4 1.6 multiply_reduce_fusion.2
  107.0 23.1 %psum.67 = f32[8192]{0:T(1024)S(1)} all-reduce(f32[8192]{0:T(1024)S(1)} %get-tuple-element.9), channel_id=1, replica_groups=mesh['data'=8] {'data'}, use_global_device_ids=true, to_apply=%region_12.13 | all-reduce | flops 8192 | bytes 65536 | tf_op jit(solution)/shard_map/psum | solution.py:14
  130.1 2.1 fusion.22
  132.3 0.0 copy-start.12
  132.3 0.7 multiply_divide_fusion.6
  133.0 0.7 copy-done.12
  133.6 0.3 multiply_reduce_fusion.7
  133.9 24.1 %psum.68 = f32[8192]{0:T(1024)S(1)} all-reduce(f32[8192]{0:T(1024)S(1)} %multiply_reduce_fusion.7), channel_id=1, replica_groups=mesh['data'=8] {'data'}, use_global_device_ids=true, to_apply=%region_15.16 | all-reduce | flops 8192 | bytes 65536 | tf_op jit(solution)/shard_map/psum | solution.py:14
  158.0 2.0 fusion.21
  160.0 0.0 copy-start.8
  160.0 0.7 multiply_divide_fusion.5
  160.7 0.7 copy-done.8
  161.4 0.3 multiply_reduce_fusion.6
  161.6 23.3 %psum.69 = f32[8192]{0:T(1024)S(1)} all-reduce(f32[8192]{0:T(1024)S(1)} %multiply_reduce_fusion.6), channel_id=1, replica_groups=mesh['data'=8] {'data'}, use_global_device_ids=true, to_apply=%region_18.19 | all-reduce | flops 8192 | bytes 65536 | tf_op jit(solution)/shard_map/psum | solution.py:14
  185.0 0.0 copy-start.9
  185.0 2.1 fusion.19
  187.1 0.7 multiply_divide_fusion.4
  187.8 0.0 copy-start.11
  187.8 1.7 multiply_convert_fusion.2
  189.6 0.0 copy-start.14
  189.6 0.0 copy-start.3
  189.6 2.8 fusion.27
  192.5 0.8 copy-done.3
  193.3 8.5 %fusion.12 = f32[10,64,8192]{2,1,0:T(8,128)} fusion(bf16[10,64,256]{2,1,0:T(8,128)(2,1)S(1)} %copy-done, bf16[8192,256]{1,0:T(8,128)(2,1)S(1)} %copy-done.3), kind=kOutput, calls=%fused_computation.16 | convolution fusion | flops 2684354560 | bytes 25493504 | tf_op jit(solution)/shard_map/jnd,kd->jnk/dot_general | solution.py:25
  201.8 21.3 %multiply_subtract_fusion = f32[10,64,8192]{2,1,0:T(8,128)} fusion(f32[10,64,8192]{2,1,0:T(8,128)} %fusion.12), kind=kOutput, calls=%fused_computation.8 | output fusion | flops 15737471 | bytes 41943040 | tf_op jit(solution)/shard_map/jit(log_softmax)/sub | solution.py:28
  223.1 19.6 %multiply_convert_fusion = (bf16[10,64,8192]{2,1,0:T(8,128)(2,1)}, f32[]{:T(128)}) fusion(f32[]{:T(128)S(6)} %div.121, f32[64]{0:T(128)S(1)} %get-tuple-element.30, f32[64,8192]{1,0:T(8,128)S(1)} %copy-done.15, f32[10,64,8192]{2,1,0:T(8,128)} %multiply_subtract_fusion), kind=kOutput, calls=%fused_computation.3 | output fusion | flops 36708992 | bytes 33554696 | tf_op jit(solution)/shard_map/jit(log_softmax)/reduce_sum | solution.py:28
  242.7 6.5 %convolution_bitcast_fusion = f32[8192,256]{1,0:T(8,128)S(1)} fusion(bf16[10,64,8192]{2,1,0:T(8,128)(2,1)} %get-tuple-element.26, bf16[10,64,256]{2,1,0:T(8,128)(2,1)S(1)} %copy-done), kind=kOutput, calls=%fused_computation.10 | convolution fusion | flops 2684354560 | bytes 19202048 | tf_op jit(solution)/shard_map/jnk,jnd->kd/dot_general | solution.py:40
  249.3 0.0 copy-start.17
  249.3 1.3 fusion.30
  250.6 4.8 %fusion.8 = f32[8192,256]{1,0:T(8,128)} fusion(f32[8192,256]{1,0:T(8,128)S(1)} %convolution_bitcast_fusion, f32[8192,256]{1,0:T(8,128)S(1)} %fusion.30, bf16[64,8192]{1,0:T(8,128)(2,1)S(1)} %copy-done.13, bf16[64,256]{1,0:T(8,128)(2,1)S(1)} %copy-done.17), kind=kOutput, calls=%fused_computation.12 | convolution fusion | flops 272629760 | bytes 26247168 | tf_op jit(solution)/shard_map/nk,nd->kd/dot_general | solution.py:39
  255.4 0.0 all-reduce.3.cloned.1.call-update
  257.4 24.7 %psum.70 = f32[]{:T(128)} all-reduce(f32[]{:T(128)S(6)} %add.35), channel_id=1, replica_groups=mesh['data'=8] {'data'}, use_global_device_ids=true, to_apply=%region_27.29 | all-reduce | flops 1 | bytes 8 | tf_op jit(solution)/shard_map/psum | solution.py:31
  283.4 0.0 copy-start.4
  283.4 3.8 fusion.28
  287.2 1.4 fusion.29
  288.6 6.4 %fusion.10 = f32[10,64,256]{2,1,0:T(8,128)} fusion(bf16[10,64,8192]{2,1,0:T(8,128)(2,1)} %get-tuple-element.26, bf16[8192,256]{1,0:T(8,128)(2,1)S(1)} %copy-done.4), kind=kOutput, calls=%fused_computation.14 | convolution fusion | flops 2684354560 | bytes 15335424 | tf_op jit(solution)/shard_map/jnk,kd->jnd/dot_general | solution.py:37
  295.0 78.3 %all-reduce.3.cloned.1.call-done = f32[8192,256]{1,0:T(8,128)} async-done(((f32[8192,256]{1,0:T(8,128)}), f32[8192,256]{1,0:T(8,128)}) %all-reduce.3.cloned.1.call-update) | async-done | bytes 8388624 | tf_op jit(solution)/shard_map/psum | solution.py:41
  373.4 7.4 %copy.13 = f32[8192,256]{1,0:T(8,128)} copy(f32[8192,256]{1,0:T(8,128)} %all-reduce.3.cloned.1.call-done) | data formatting | bytes 16777216
  (28 shorter events, 0.1 us)
Async XLA Ops:
  7.2 185.3 %copy-start = (bf16[10,64,256]{2,1,0:T(8,128)(2,1)S(1)}, bf16[10,64,256]{2,1,0:T(8,128)(2,1)}, u32[]{:S(2)}) copy-start(bf16[10,64,256]{2,1,0:T(8,128)(2,1)} %param.8) | copy-start | bytes 983044
  7.2 366.2 %all-reduce.3.cloned.1.call-start = ((), (), s32[]{:S(2)}) async-start(), calls=%async_computation | async-start | bytes 16777216 | tf_op jit(solution)/shard_map/psum | solution.py:41
  9.2 4.4 %copy-start.2 = (bf16[8192,256]{1,0:T(8,128)(2,1)S(1)}, bf16[8192,256]{1,0:T(8,128)(2,1)}, u32[]{:S(2)}) copy-start(bf16[8192,256]{1,0:T(8,128)(2,1)} %param.9) | copy-start | bytes 12582916
  13.0 2.3 copy-start.5
  13.1 0.8 copy-start.16
  41.8 2.5 copy-start.18
  72.0 1.3 copy-start.7
  100.4 5.0 %copy-start.6 = (f32[64,8192]{1,0:T(8,128)S(1)}, f32[64,8192]{1,0:T(8,128)}, u32[]{:S(2)}) copy-start(f32[64,8192]{1,0:T(8,128)} %copy-done.5) | copy-start | bytes 6291460
  105.4 1.6 copy-start.10
  132.3 1.3 copy-start.12
  160.0 1.3 copy-start.8
  185.0 2.8 copy-start.9
  187.8 1.8 copy-start.11
  189.6 2.9 copy-start.14
  189.6 3.7 copy-start.3
  201.8 21.3 %copy-start.15 = (f32[64,8192]{1,0:T(8,128)S(1)}, f32[64,8192]{1,0:T(8,128)}, u32[]{:S(2)}) copy-start(f32[64,8192]{1,0:T(8,128)} %get-tuple-element.28) | copy-start | bytes 6291460
  249.3 1.3 copy-start.13
  249.3 1.3 copy-start.17
  283.4 3.8 copy-start.4
  373.4 7.4 %copy-start.1 = (bf16[10,64,256]{2,1,0:T(8,128)(2,1)S(1)}, bf16[10,64,256]{2,1,0:T(8,128)(2,1)}, u32[]{:S(2)}) copy-start(bf16[10,64,256]{2,1,0:T(8,128)(2,1)} %param.8) | copy-start | bytes 983044
Sparse Core Ops, SparseCore 0:
  255.5 117.7 all-reduce.2
where the time goes:
time: 390 us; the launch traced here: 389 us
  blocking collectives  168 us (43%)
  waiting for transfers between devices  78.3 us (20%)
  other arithmetic  74.1 us (19%)
  matrix products  38.1 us (10%)
  between operations  19.5 us (5%)
  local copies, waits for them, and re-layouts  10.5 us (3%)
    psum x6, blocking collectives, value_a14(): col_sum = lax.psum(jnp.sum(weights, axis=0), 'data')  143 us
    psum x1, waiting for transfers between devices, loss_and_grads(): d_protos = lax.psum(dc_part, 'data')  78.3 us
    psum x1, blocking collectives, loss_and_grads(): loss_total = -lax.psum(cross_sum, 'data') / (live_total * pair_count)  24.7 us
    sub x1, other arithmetic, loss_and_grads(): logp_small = jax.nn.log_softmax(scores_small / TAU, axis=-1)  21.3 us
    reduce_sum x1, other arithmetic, loss_and_grads(): logp_small = jax.nn.log_softmax(scores_small / TAU, axis=-1)  19.6 us
    reduce_sum x6, other arithmetic, value_a14(): row_sum = jnp.sum(weights, axis=1, keepdims=True)  12.1 us
    unnamed x39, local copies, waits for them, and re-layouts  10.5 us
    dot_general x1, matrix products, loss_and_grads(): jnp.einsum('jnd,kd->jnk', z_small, protos, preferred_element_type=jnp.flo...  8.53 us
  transfers between devices with their start and end apart: 1, of which 1 were waited for; matrix products, arithmetic and copies ran while one was open for 3% of the time, Pallas kernels for 0%

commit v1 on v0

v1 whole, which is shorter than its diff:
```python
import functools
import math

import jax
import jax.numpy as jnp
from jax import lax
from jax.experimental import pallas as pl
from jax.experimental.pallas import tpu as pltpu
from jax.sharding import PartitionSpec as P

EPS = 0.05
TAU = 0.1
ITERS = 3
DEVS = 8
ROWS = 64
NROW = ROWS * DEVS
PROTOS = 8192
DIM = 256
VIEWS = 12
OWN = PROTOS // DEVS
KC = 256
NCH = OWN // KC
PC = 512
MESH = pl.DeviceIdType.MESH
F32 = jnp.float32
BF16 = jnp.bfloat16
UNITS = ((0, 1), (1, 1), (2, 4), (6, 3), (9, 3))


def nt_dot(a, b):
    return lax.dot_general(a, b, (((1,), (1,)), ((), ())), preferred_element_type=F32)


def body(mask_ref, z1_ref, z2_ref, zs_ref, c_hbm,
         q1_hbm, q2_hbm, loss_ref, dz1_ref, dz2_ref, dzs_ref, dc_hbm,
         zall, zown, cv, et, a0, gq, gt, dcv, qbuf, vb, vx, rx, lx, mx, px,
         mvec, wvec, acf, cf, ct, ab, ssum_ref, dzacc,
         csem, zsend, zrecv, rsend, rrecv, lsend, lrecv, vsend, vrecv, psend, precv,
         asend, arecv, qsem, osem):
    me = lax.axis_index("data")
    core = me % 2
    xpos = (me // 2) % 2
    ypos = me // 4
    partner = me + 1 - 2 * core
    xn = me + 2 - 4 * xpos
    yn = me + 4 - 8 * ypos
    dg = xn + 4 - 8 * ypos

    def other(d):
        return d + 1 - 2 * core

    own0 = pl.multiple_of(me * OWN, OWN)
    c_own_copy = pltpu.make_async_copy(c_hbm.at[pl.ds(own0, OWN)], cv.at[pl.ds(own0, OWN)], csem.at[0])
    c_own_copy.start()

    barrier = pltpu.get_barrier_semaphore()
    for off in range(1, DEVS):
        pl.semaphore_signal(barrier, inc=1, device_id=((me + off) % DEVS,), device_id_type=MESH)

    mrow = mask_ref[...].astype(F32)
    sel = (lax.broadcasted_iota(jnp.int32, (ROWS, 128), 1)
           == lax.broadcasted_iota(jnp.int32, (ROWS, 128), 0) + ROWS * core)
    mplaced = jnp.dot(jnp.broadcast_to(mrow, (8, ROWS)).astype(BF16), sel.astype(BF16),
                      preferred_element_type=F32)
    mx[me] = mplaced[0:1, :]

    def zdst(unit, dev):
        lo, cnt = UNITS[unit]
        rows = pl.ds(pl.multiple_of(dev * ROWS, ROWS), ROWS)
        if cnt == 1:
            return zall.at[lo, rows]
        return zall.at[pl.ds(lo, cnt), rows]

    def zsrc(unit):
        lo, cnt = UNITS[unit]
        if unit == 0:
            return z1_ref
        if unit == 1:
            return z2_ref
        return zs_ref.at[pl.ds(lo - 2, cnt)]

    peers = (partner, xn, yn, dg)

    def zcopy(unit, kind):
        if kind < 4:
            return pltpu.make_async_remote_copy(
                src_ref=zsrc(unit), dst_ref=zdst(unit, me), send_sem=zsend.at[kind, unit],
                recv_sem=zrecv.at[kind, unit], device_id=(peers[kind],), device_id_type=MESH)
        dev = peers[kind - 3]
        return pltpu.make_async_remote_copy(
            src_ref=zdst(unit, dev), dst_ref=zdst(unit, dev), send_sem=zsend.at[kind, unit],
            recv_sem=zrecv.at[kind, unit], device_id=(partner,), device_id_type=MESH)

    def zwait(unit, kind):
        dev = peers[kind] if kind < 4 else other(peers[kind - 3])
        pltpu.make_async_remote_copy(
            src_ref=zsrc(unit), dst_ref=zdst(unit, dev), send_sem=zsend.at[kind, unit],
            recv_sem=zrecv.at[kind, unit], device_id=(partner,), device_id_type=MESH).wait_recv()

    def zstart(unit):
        for kind in (1, 2, 3, 0):
            zcopy(unit, kind).start()

    def zforward(units):
        for kind in (1, 2, 3):
            for unit in units:
                zwait(unit, kind)
                zcopy(unit, kind + 3).start()

    def zfinish(units):
        for unit in units:
            zwait(unit, 0)
        for kind in (4, 5, 6):
            for unit in units:
                zwait(unit, kind)

    def bcast(ref_of, send_sem, recv_sem, wait):
        for off in range(1, DEVS):
            dev = (me + off) % DEVS
            slot = dev if wait else me
            copy = pltpu.make_async_remote_copy(
                src_ref=ref_of(slot), dst_ref=ref_of(slot), send_sem=send_sem(off),
                recv_sem=recv_sem(slot), device_id=(dev,), device_id_type=MESH)
            if wait:
                copy.wait_recv()
            else:
                copy.start()

    def bcast_drain(ref_of, send_sem, recv_sem):
        for off in range(1, DEVS):
            pltpu.make_async_remote_copy(
                src_ref=ref_of(me), dst_ref=ref_of(me), send_sem=send_sem(off),
                recv_sem=recv_sem(me), device_id=((me + off) % DEVS,), device_id_type=MESH).wait_send()

    m_args = (lambda d: mx.at[d], lambda o: psend.at[1, o], lambda d: precv.at[1, d])
    p_args = (lambda d: px.at[d], lambda o: psend.at[0, o], lambda d: precv.at[0, d])
    v_args = (lambda d: vx.at[d], lambda o: vsend.at[o], lambda d: vrecv.at[d])

    def r_args(step):
        return (lambda d: rx.at[step, d], lambda o: rsend.at[step, o], lambda d: rrecv.at[step, d])

    def l_args(part):
        lo, cnt = ((0, 6), (6, 6))[part]
        return (lambda d: lx.at[d, pl.ds(lo, cnt)], lambda o: lsend.at[part, o], lambda d: lrecv.at[part, d])

    my_rows = pl.ds(pl.multiple_of(me * ROWS, ROWS), ROWS)
    zall[0, my_rows] = z1_ref[...]
    zall[1, my_rows] = z2_ref[...]
    zown[0] = z1_ref[...]
    zown[1] = z2_ref[...]
    for view in range(VIEWS - 2):
        zall[2 + view, my_rows] = zs_ref[view]
        zown[2 + view] = zs_ref[view]

    pl.semaphore_wait(barrier, DEVS - 1)
    zstart(0)
    zstart(1)
    bcast(*m_args, wait=False)
    zstart(2)

    c_copies = []
    for off in range(1, DEVS):
        lo = pl.multiple_of(((me + off) % DEVS) * OWN, OWN)
        c_copies.append(pltpu.make_async_copy(c_hbm.at[pl.ds(lo, OWN)], cv.at[pl.ds(lo, OWN)], csem.at[off]))
        c_copies[-1].start()
    c_own_copy.wait()

    def exp_block(view, ch):
        rows = pl.ds(pl.multiple_of(ch * KC, KC), KC)
        scores = nt_dot(cv[pl.ds(pl.multiple_of(own0 + ch * KC, KC), KC)], zall[view])
        e = jnp.exp(scores * (1.0 / TAU))
        et[view, rows] = e
        return rows, e

    def fold(x):
        return jnp.sum(x.reshape(x.shape[0] // 8, 8, x.shape[1]), axis=0)

    def exp_view(view):
        def step(ch, acc):
            _, e = exp_block(view, ch)
            return acc + fold(e)
        acc = lax.fori_loop(0, NCH, step, jnp.zeros((8, NROW), F32))
        lx[me, view] = jnp.sum(acc, axis=0, keepdims=True)

    def exp_views(lo, hi):
        def step(view, carry):
            exp_view(view)
            return carry
        lax.fori_loop(lo, hi, step, 0)

    zforward((0, 1))
    bcast(*m_args, wait=True)
    zfinish((0, 1))
    for q in range(NROW // 128):
        mvec[:, q * 128:(q + 1) * 128] = mx[2 * q] + mx[2 * q + 1]
    live_total = jnp.sum(mvec[...], axis=1, keepdims=True)

    SB = 64

    for view in range(2):
        def step(ch, acc):
            rows, e = exp_block(view, ch)
            a0[view, rows] = e * e
            return acc + fold(e)
        acc = lax.fori_loop(0, NCH, step, jnp.zeros((8, NROW), F32))
        lx[me, view] = jnp.sum(acc, axis=0, keepdims=True)

    def sink_pass(it):
        for view in range(2):
            scale = (1.0 if it == 0 else live_total) * (1.0 / PROTOS)

            def step(blk, acc):
                rows = pl.ds(pl.multiple_of(blk * SB, SB), SB)
                a = a0[view, rows]
                w = mvec[...] if it == 0 else wvec[view]
                colsum = jnp.sum(a * w, axis=1, keepdims=True)
                v = scale / colsum
                if it == ITERS - 1:
                    vb[view, rows] = jnp.broadcast_to(v, (SB, 128))
                return acc + fold(a * v)
            acc = lax.fori_loop(0, OWN // SB, step, jnp.zeros((8, NROW), F32))
            rx[it, me, :, view * NROW:(view + 1) * NROW] = jnp.sum(acc, axis=0, keepdims=True)
        bcast(*r_args(it), wait=False)

    def sink_close(it):
        bcast(*r_args(it), wait=True)
        tot = rx[it, 0]
        for d in range(1, DEVS):
            tot = tot + rx[it, d]
        for view in range(2):
            wvec[view] = mvec[...] / tot[:, view * NROW:(view + 1) * NROW]

    sink_pass(0)
    zstart(3)
    zforward((2,))
    zfinish((2,))
    exp_views(2, 6)
    bcast(*l_args(0), wait=False)
    sink_close(0)
    sink_pass(1)
    zstart(4)
    zforward((3,))
    zfinish((3,))
    exp_views(6, 9)
    sink_close(1)
    sink_pass(2)
    zforward((4,))
    zfinish((4,))
    exp_views(9, 12)
    bcast(*l_args(1), wait=False)

    for view in range(2):
        for blk in range(OWN // 128):
            vt = vb[view, blk * 128:(blk + 1) * 128].T
            vx[me, view, :, blk * 128:(blk + 1) * 128] = vt[0:1, :]
    bcast(*v_args, wait=False)

    sink_close(2)
    bcast(*l_args(0), wait=True)
    bcast(*l_args(1), wait=True)
    grad_scale = 1.0 / (TAU * live_total * (2 + 2 * (VIEWS - 2)))
    log_sum = jnp.zeros((1, NROW), F32)
    for view in range(VIEWS):
        tot = lx[0, view]
        for d in range(1, DEVS):
            tot = tot + lx[d, view]
        mult = 1.0 if view < 2 else 2.0
        acf[view] = (mult * grad_scale) * mvec[...] / tot
        log_sum = log_sum + mult * jnp.log(tot)
    log_sum = jnp.sum(log_sum * mvec[...], axis=1, keepdims=True)

    def acopy(src_dev, ch, half, to, kind):
        lo = src_dev * OWN + ch * KC
        if half is None:
            rows = pl.ds(pl.multiple_of(lo, KC), KC)
        else:
            rows = pl.ds(pl.multiple_of(lo + half * (KC // 2), KC // 2), KC // 2)
        return pltpu.make_async_remote_copy(
            src_ref=dcv.at[rows], dst_ref=dcv.at[rows], send_sem=asend.at[kind, ch],
            recv_sem=arecv.at[kind, ch], device_id=(to,), device_id_type=MESH)

    def dc_chunk(ch, carry):
        rows = pl.ds(pl.multiple_of(ch * KC, KC), KC)
        for view in range(2):
            v = vb[view, rows]
            v = jnp.concatenate([v] * (NROW // 128), axis=1)
            gq[view] = (wvec[view] * grad_scale) * (v * a0[view, rows])
        gq[2] = gq[0] + gq[1]
        g0 = (acf[0] * et[0, rows] - gq[1]).astype(BF16)
        acc = jnp.dot(g0, zall[0], preferred_element_type=F32)
        g1 = (acf[1] * et[1, rows] - gq[0]).astype(BF16)
        acc = acc + jnp.dot(g1, zall[1], preferred_element_type=F32)

        def step(view, acc):
            g = (acf[view] * et[view, rows] - gq[2]).astype(BF16)
            return acc + jnp.dot(g, zall[view], preferred_element_type=F32)
        acc = lax.fori_loop(2, VIEWS, step, acc)
        dcv[pl.ds(pl.multiple_of(own0 + ch * KC, KC), KC)] = acc
        for kind, to in ((0, xn), (1, yn), (2, partner)):
            acopy(me, ch, None, to, kind).start()
        return carry
    lax.fori_loop(0, NCH, dc_chunk, 0)

    lanes = pl.ds(pl.multiple_of((me // 2) * 128, 128), 128)
    for view in range(VIEWS):
        cf[view:view + 1, :] = acf[view, :, lanes]
    for view in range(2):
        cf[VIEWS + view:VIEWS + view + 1, :] = wvec[view, :, lanes]
    ct[...] = cf[...].T
    own_cf = ct[pl.ds(pl.multiple_of(core * ROWS, ROWS), ROWS), :]
    for j in range(VIEWS + 2):
        ab[j] = jnp.broadcast_to(own_cf[:, j:j + 1], (ROWS, 128))

    for copy in c_copies:
        copy.wait()
    bcast(*v_args, wait=True)
    dzacc[...] = jnp.zeros_like(dzacc)

    def wide(x):
        return jnp.concatenate([x] * (PC // 128), axis=1)

    def qcopy(view, ch, slot):
        cols = pl.ds(pl.multiple_of(ch * PC, PC), PC)
        return pltpu.make_async_copy(qbuf.at[slot, view], (q1_hbm, q2_hbm)[view].at[:, cols], qsem.at[slot, view])

    def row_chunk(ch, acc):
        slot = ch % 2

        @pl.when(ch >= 2)
        def _():
            for view in range(2):
                qcopy(view, ch - 2, slot).wait()
        cc = cv[pl.ds(pl.multiple_of(ch * PC, PC), PC)]
        scores = nt_dot(zown[...].reshape(VIEWS * ROWS, DIM), cc)
        dev = ch // (OWN // PC)
        half = pl.ds(pl.multiple_of((ch % (OWN // PC)) * PC, PC), PC)
        e_large, q_large = [], []
        for view in range(2):
            e = jnp.exp(scores[view * ROWS:(view + 1) * ROWS] * (1.0 / TAU))
            q = wide(ab[VIEWS + view]) * (vx[dev, view, :, half] * (e * e))
            qbuf[slot, view] = q
            e_large.append(e)
            q_large.append(q)
        q_sum = q_large[0] + q_large[1]
        gq_sum = q_sum * grad_scale
        parts = [(wide(ab[0]) * e_large[0] - q_large[1] * grad_scale).astype(BF16),
                 (wide(ab[1]) * e_large[1] - q_large[0] * grad_scale).astype(BF16)]
        s_sum = None
        for view in range(2, VIEWS):
            s = scores[view * ROWS:(view + 1) * ROWS]
            s_sum = s if s_sum is None else s_sum + s
            parts.append((wide(ab[view]) * jnp.exp(s * (1.0 / TAU)) - gq_sum).astype(BF16))
        dot = q_large[1] * scores[0:ROWS] + q_large[0] * scores[ROWS:2 * ROWS] + q_sum * s_sum
        for view in range(2):
            qcopy(view, ch, slot).start()
        dzacc[...] += jnp.dot(jnp.concatenate(parts, axis=0), cc, preferred_element_type=F32)
        return acc + fold(dot)
    acc = lax.fori_loop(0, PROTOS // PC, row_chunk, jnp.zeros((8, PC), F32))
    cross = jnp.sum(jnp.sum(acc, axis=0, keepdims=True), axis=1, keepdims=True)
    px[me] = jnp.broadcast_to(cross, (1, 128))
    bcast(*p_args, wait=False)
    dz1_ref[...] = dzacc[0:ROWS]
    dz2_ref[...] = dzacc[ROWS:2 * ROWS]
    for view in range(VIEWS - 2):
        dzs_ref[view] = dzacc[(view + 2) * ROWS:(view + 3) * ROWS]

    def out_copy(dev, ch, half, kind):
        lo = dev * OWN + ch * KC
        if half is None:
            rows = pl.ds(pl.multiple_of(lo, KC), KC)
        else:
            rows = pl.ds(pl.multiple_of(lo + half * (KC // 2), KC // 2), KC // 2)
        return pltpu.make_async_copy(dcv.at[rows], dc_hbm.at[rows], osem.at[kind, ch])

    def gather_near(ch, carry):
        acopy(xn, ch, None, xn, 0).wait_recv()
        acopy(xn, ch, 0, yn, 3).start()
        acopy(xn, ch, None, partner, 5).start()
        acopy(yn, ch, None, yn, 1).wait_recv()
        acopy(yn, ch, 1, xn, 4).start()
        acopy(yn, ch, None, partner, 6).start()
        out_copy(me, ch, None, 0).start()
        out_copy(xn, ch, None, 1).start()
        out_copy(yn, ch, None, 2).start()
        acopy(partner, ch, None, partner, 2).wait_recv()
        out_copy(partner, ch, None, 3).start()
        return carry

    def gather_far(ch, carry):
        acopy(dg, ch, 0, yn, 3).wait_recv()
        acopy(dg, ch, 0, partner, 7).start()
        acopy(dg, ch, 1, xn, 4).wait_recv()
        acopy(dg, ch, 1, partner, 8).start()
        out_copy(dg, ch, None, 4).start()
        acopy(other(xn), ch, None, partner, 5).wait_recv()
        out_copy(other(xn), ch, None, 5).start()
        acopy(other(yn), ch, None, partner, 6).wait_recv()
        out_copy(other(yn), ch, None, 6).start()
        acopy(other(dg), ch, 0, partner, 7).wait_recv()
        acopy(other(dg), ch, 1, partner, 8).wait_recv()
        out_copy(other(dg), ch, None, 7).start()
        return carry
    lax.fori_loop(0, NCH, gather_near, 0)
    bcast(*p_args, wait=True)
    tot = px[0]
    for d in range(1, DEVS):
        tot = tot + px[d]
    loss = -(tot[:, 0:1] * (1.0 / TAU) - log_sum) / (live_total * (2 + 2 * (VIEWS - 2)))
    loss_ref[...] = jnp.broadcast_to(loss, (1, 128))
    lax.fori_loop(0, NCH, gather_far, 0)

    def drain(ch, carry):
        for kind in (0, 1, 2):
            acopy(me, ch, None, partner, kind).wait_send()
        acopy(xn, ch, 0, yn, 3).wait_send()
        acopy(yn, ch, 1, xn, 4).wait_send()
        acopy(xn, ch, None, partner, 5).wait_send()
        acopy(yn, ch, None, partner, 6).wait_send()
        acopy(dg, ch, 0, partner, 7).wait_send()
        acopy(dg, ch, 1, partner, 8).wait_send()
        for kind, dev in enumerate((me, xn, yn, partner, dg, other(xn), other(yn), other(dg))):
            out_copy(dev, ch, None, kind).wait()
        return carry
    for unit in range(len(UNITS)):
        for kind in range(7):
            zcopy(unit, kind).wait_send()
    bcast_drain(*m_args)
    bcast_drain(*p_args)
    bcast_drain(*v_args)
    for it in range(ITERS):
        bcast_drain(*r_args(it))
    for part in range(2):
        bcast_drain(*l_args(part))
    for ch in (PROTOS // PC - 2, PROTOS // PC - 1):
        for view in range(2):
            qcopy(view, ch, ch % 2).wait()
    lax.fori_loop(0, NCH, drain, 0)


def local_step(z_one, z_two, z_small, protos, live_mask):
    vmem = pl.BlockSpec(memory_space=pltpu.VMEM)
    hbm = pl.BlockSpec(memory_space=pl.ANY)
    dma = pltpu.SemaphoreType.DMA
    views = VIEWS
    out = pl.pallas_call(
        body,
        out_shape=(
            jax.ShapeDtypeStruct((ROWS, PROTOS), F32),
            jax.ShapeDtypeStruct((ROWS, PROTOS), F32),
            jax.ShapeDtypeStruct((1, 128), F32),
            jax.ShapeDtypeStruct((ROWS, DIM), F32),
            jax.ShapeDtypeStruct((ROWS, DIM), F32),
            jax.ShapeDtypeStruct((views - 2, ROWS, DIM), F32),
            jax.ShapeDtypeStruct((PROTOS, DIM), F32),
        ),
        in_specs=[vmem, vmem, vmem, vmem, hbm],
        out_specs=(hbm, hbm, vmem, vmem, vmem, vmem, hbm),
        scratch_shapes=[
            pltpu.VMEM((views, NROW, DIM), BF16),
            pltpu.VMEM((views, ROWS, DIM), BF16),
            pltpu.VMEM((PROTOS, DIM), BF16),
            pltpu.VMEM((views, OWN, NROW), F32),
            pltpu.VMEM((2, OWN, NROW), F32),
            pltpu.VMEM((3, KC, NROW), F32),
            pltpu.VMEM((8, 128), BF16),
            pltpu.VMEM((PROTOS, DIM), F32),
            pltpu.VMEM((2, 2, ROWS, PC), F32),
            pltpu.VMEM((2, OWN, 128), F32),
            pltpu.VMEM((DEVS, 2, 1, OWN), F32),
            pltpu.VMEM((ITERS, DEVS, 1, 2 * NROW), F32),
            pltpu.VMEM((DEVS, views, 1, NROW), F32),
            pltpu.VMEM((DEVS, 1, 128), F32),
            pltpu.VMEM((DEVS, 1, 128), F32),
            pltpu.VMEM((1, NROW), F32),
            pltpu.VMEM((2, 1, NROW), F32),
            pltpu.VMEM((views, 1, NROW), F32),
            pltpu.VMEM((128, 128), F32),
            pltpu.VMEM((128, 128), F32),
            pltpu.VMEM((views + 2, ROWS, 128), F32),
            pltpu.VMEM((8, 128), F32),
            pltpu.VMEM((views * ROWS, DIM), F32),
            dma((DEVS,)),
            dma((7, 5)), dma((7, 5)),
            dma((ITERS, DEVS)), dma((ITERS, DEVS)),
            dma((2, DEVS)), dma((2, DEVS)),
            dma((DEVS,)), dma((DEVS,)),
            dma((2, DEVS)), dma((2, DEVS)),
            dma((9, NCH)), dma((9, NCH)),
            dma((2, 2)),
            dma((8, NCH)),
        ],
        compiler_params=pltpu.CompilerParams(
            collective_id=0, has_side_effects=True, vmem_limit_bytes=62 * 1024 * 1024),
        name="swav_step",
    )(live_mask.reshape(1, ROWS), z_one, z_two, z_small, protos)
    q_one, q_two, loss, dz_one, dz_two, dz_small, d_protos = out
    return q_one, q_two, loss[0, 0], dz_one, dz_two, dz_small, d_protos


def solution(mesh):
    row_spec = P("data", None)
    crop_spec = P(None, "data", None)
    return jax.shard_map(local_step, mesh=mesh,
                         in_specs=(row_spec, row_spec, crop_spec, P(None, None), P("data")),
                         out_specs=(row_spec, row_spec, P(), row_spec, row_spec, crop_spec, P(None, None)),
                         check_vma=False)
```

time: 390 us -> 103 us (0.26)
  blocking collectives: 168 us -> 0 us
  Pallas kernels: 0 us -> 86.7 us
  waiting for transfers between devices: 78.3 us -> 0 us
  other arithmetic: 74.1 us -> 0 us
  matrix products: 38.1 us -> 0 us
  between operations: 19.5 us -> 1.85 us
    psum x7 -> x0, blocking collectives: 168 us -> none  [the longest x6 143 us: value_a14(): col_sum = lax.psum(jnp.sum(weights, axis=0), 'data')]
    pallas_call x0 -> x1, Pallas kernels: none -> 86.7 us  [local_step(): pl.pallas_call(body, out_shape=(jax.ShapeDtypeStruct((ROWS, PROTOS), F32)...]
    psum x1 -> x0, waiting for transfers between devices: 78.3 us -> none  [loss_and_grads(): d_protos = lax.psum(dc_part, 'data')]
    dot_general x9 -> x0, matrix products: 38.1 us -> none  [the longest x1 8.53 us: loss_and_grads(): jnp.einsum('jnd,kd->jnk', z_small, protos, preferred_element_type=jnp.flo...]
    reduce_sum x14 -> x0, other arithmetic: 37.3 us -> none  [the longest x1 19.6 us: loss_and_grads(): logp_small = jax.nn.log_softmax(scores_small / TAU, axis=-1)]
    sub x1 -> x0, other arithmetic: 21.3 us -> none  [loss_and_grads(): logp_small = jax.nn.log_softmax(scores_small / TAU, axis=-1)]
    convert_element_type x3 -> x0, other arithmetic: 7.41 us -> none  [the longest x1 4.97 us: loss_and_grads(): ((live_col * jnp.exp(logp_two) - q_one) * grad_scale).astype(jnp.bfloat16)]
    div x6 -> x0, other arithmetic: 3.94 us -> none  [value_a14(): weights = weights * (live_col / (live_total * row_safe))]
  transfers between devices with their start and end apart: 1 -> 0, of which waited for: 1 -> 0; matrix products, arithmetic and copies ran while one was open for 3% -> 0% of each run, Pallas kernels for 0% -> 0%
where the time goes in v1:
time: 103 us; the launch traced here: 102 us
  Pallas kernels  86.7 us (84%)
  local copies, waits for them, and re-layouts  14 us (14%)
  between operations  1.85 us (2%)
    pallas_call x1, Pallas kernels, local_step(): pl.pallas_call(body, out_shape=(jax.ShapeDtypeStruct((ROWS, PROTOS), F32)...  86.7 us
    unnamed x16, local copies, waits for them, and re-layouts  14 us

profile of v1, /device:TPU:0, one launch (start us, length us, event | category | flops | bytes accessed | tf_op | source)
XLA Modules:
  0.0 102.5 jit_solution(17102997637249200051)
XLA Ops:
  0.6 86.7 %swav_step.1 = (f32[64,8192]{1,0:T(8,128)}, f32[64,8192]{1,0:T(8,128)}, f32[1,128]{1,0:T(1,128)}, f32[64,256]{1,0:T(8,128)}, f32[64,256]{1,0:T(8,128)}, /*index=5*/f32[10,64,256]{2,1,0:T(8,128)}, f32[8192,256]{1,0:T(8,128)}) custom-call(s32[1,64]{1,0:T(1,128)} %bitcast.3, bf16[64,256]{1,0:T(8,128)(2,1)} %z1_ref.1, bf16[64,256]{1,0:T(8,128)(2,1)} %z2_ref.1, ...), custom_call_target="tpu_custom_call" | custom-call | tf_op jit(solution)/shard_map/swav_step/pallas_call | solution.py:445
  87.3 0.0 copy-start
  87.3 3.2 %copy.19 = f32[64,8192]{1,0:T(8,128)} copy(f32[64,8192]{1,0:T(8,128)} %get-tuple-element.28) | data formatting | bytes 4194304
  90.5 0.0 copy-done
  90.5 0.0 copy-start.4
  90.5 0.0 copy-start.3
  90.5 0.0 copy-start.2
  90.6 0.0 copy-start.1
  90.6 1.3 %copy.20 = f32[64,8192]{1,0:T(8,128)} copy(f32[64,8192]{1,0:T(8,128)S(1)} %copy-done) | data formatting | bytes 4194304
  91.9 0.0 copy-done.4
  91.9 0.0 copy-done.3
  91.9 0.6 copy.22
  92.6 0.0 copy-done.2
  92.6 0.6 copy.23
  93.2 0.0 copy-done.1
  93.2 0.8 copy.24
  94.0 7.3 %copy.25 = f32[8192,256]{1,0:T(8,128)} copy(f32[8192,256]{1,0:T(8,128)} %get-tuple-element.34) | data formatting | bytes 16777216
Async XLA Ops:
  87.3 3.2 %copy-start = (f32[64,8192]{1,0:T(8,128)S(1)}, f32[64,8192]{1,0:T(8,128)}, u32[]{:S(2)}) copy-start(f32[64,8192]{1,0:T(8,128)} %get-tuple-element.29) | copy-start | bytes 6291460
  90.5 1.3 %copy-start.4 = (f32[1,128]{1,0:T(1,128)S(1)}, f32[1,128]{1,0:T(1,128)}, u32[]{:S(2)}) copy-start(f32[1,128]{1,0:T(1,128)} %get-tuple-element.16) | copy-start | bytes 1540
  90.5 1.4 %copy-start.3 = (f32[64,256]{1,0:T(8,128)S(1)}, f32[64,256]{1,0:T(8,128)}, u32[]{:S(2)}) copy-start(f32[64,256]{1,0:T(8,128)} %get-tuple-element.31) | copy-start | bytes 196612
  90.5 2.0 %copy-start.2 = (f32[64,256]{1,0:T(8,128)S(1)}, f32[64,256]{1,0:T(8,128)}, u32[]{:S(2)}) copy-start(f32[64,256]{1,0:T(8,128)} %get-tuple-element.32) | copy-start | bytes 196612
  90.6 2.7 %copy-start.1 = (f32[10,64,256]{2,1,0:T(8,128)S(1)}, f32[10,64,256]{2,1,0:T(8,128)}, u32[]{:S(2)}) copy-start(f32[10,64,256]{2,1,0:T(8,128)} %get-tuple-element.33) | copy-start | bytes 1966084

commit v2 on v1

--- a/solution.py
+++ b/solution.py
@@ -32,11 +32,11 @@
 
 
 def body(mask_ref, z1_ref, z2_ref, zs_ref, c_hbm,
-         q1_hbm, q2_hbm, loss_ref, dz1_ref, dz2_ref, dzs_ref, dc_hbm,
-         zall, zown, cv, et, a0, gq, gt, dcv, qbuf, vb, vx, rx, lx, mx, px,
-         mvec, wvec, acf, cf, ct, ab, ssum_ref, dzacc,
+         q_out, loss_ref, dz_out, dcv,
+         zall, zown, cv, et, a0, vb, vx, rx, lx, mx, px,
+         mvec, wvec, acf, cf, ct, ab, lacc,
          csem, zsend, zrecv, rsend, rrecv, lsend, lrecv, vsend, vrecv, psend, precv,
-         asend, arecv, qsem, osem):
+         asend, arecv):
     me = lax.axis_index("data")
     core = me % 2
     xpos = (me // 2) % 2
@@ -50,8 +50,8 @@
         return d + 1 - 2 * core
 
     own0 = pl.multiple_of(me * OWN, OWN)
-    c_own_copy = pltpu.make_async_copy(c_hbm.at[pl.ds(own0, OWN)], cv.at[pl.ds(own0, OWN)], csem.at[0])
-    c_own_copy.start()
+    c_copy = pltpu.make_async_copy(c_hbm, cv, csem)
+    c_copy.start()
 
     barrier = pltpu.get_barrier_semaphore()
     for off in range(1, DEVS):
@@ -139,9 +139,7 @@
     def r_args(step):
         return (lambda d: rx.at[step, d], lambda o: rsend.at[step, o], lambda d: rrecv.at[step, d])
 
-    def l_args(part):
-        lo, cnt = ((0, 6), (6, 6))[part]
-        return (lambda d: lx.at[d, pl.ds(lo, cnt)], lambda o: lsend.at[part, o], lambda d: lrecv.at[part, d])
+    l_args = (lambda d: lx.at[d], lambda o: lsend.at[o], lambda d: lrecv.at[d])
 
     my_rows = pl.ds(pl.multiple_of(me * ROWS, ROWS), ROWS)
     zall[0, my_rows] = z1_ref[...]
@@ -158,12 +156,28 @@
     bcast(*m_args, wait=False)
     zstart(2)
 
-    c_copies = []
-    for off in range(1, DEVS):
-        lo = pl.multiple_of(((me + off) % DEVS) * OWN, OWN)
-        c_copies.append(pltpu.make_async_copy(c_hbm.at[pl.ds(lo, OWN)], cv.at[pl.ds(lo, OWN)], csem.at[off]))
-        c_copies[-1].start()
-    c_own_copy.wait()
+    def fold(x):
+        return jnp.sum(x.reshape(x.shape[0] // 8, 8, x.shape[1]), axis=0)
+
+    def lane_fold(x):
+        out = x[:, 0:128]
+        for i in range(1, x.shape[1] // 128):
+            out = out + x[:, i * 128:(i + 1) * 128]
+        return out
+
+    lacc[...] = jnp.zeros_like(lacc)
+    c_copy.wait()
+
+    def sum_chunk(ch, carry):
+        cc = cv[pl.ds(pl.multiple_of(ch * PC, PC), PC)]
+        scores = nt_dot(zown[...].reshape(VIEWS * ROWS, DIM), cc)
+        lacc[...] += lane_fold(jnp.exp(scores * (1.0 / TAU)))
+        return carry
+    lax.fori_loop(0, PROTOS // PC, sum_chunk, 0)
+    for view in range(VIEWS):
+        la = lacc[view * ROWS:(view + 1) * ROWS]
+        lx[me, view] = jnp.sum(jnp.concatenate([la, la], axis=0).T, axis=0, keepdims=True)
+    bcast(*l_args, wait=False)
 
     def exp_block(view, ch):
         rows = pl.ds(pl.multiple_of(ch * KC, KC), KC)
@@ -172,21 +186,11 @@
         et[view, rows] = e
         return rows, e
 
-    def fold(x):
-        return jnp.sum(x.reshape(x.shape[0] // 8, 8, x.shape[1]), axis=0)
-
-    def exp_view(view):
-        def step(ch, acc):
-            _, e = exp_block(view, ch)
-            return acc + fold(e)
-        acc = lax.fori_loop(0, NCH, step, jnp.zeros((8, NROW), F32))
-        lx[me, view] = jnp.sum(acc, axis=0, keepdims=True)
-
     def exp_views(lo, hi):
-        def step(view, carry):
-            exp_view(view)
+        def step(i, carry):
+            exp_block(lo + i // NCH, i % NCH)
             return carry
-        lax.fori_loop(lo, hi, step, 0)
+        lax.fori_loop(0, (hi - lo) * NCH, step, 0)
 
     zforward((0, 1))
     bcast(*m_args, wait=True)
@@ -195,31 +199,34 @@
         mvec[:, q * 128:(q + 1) * 128] = mx[2 * q] + mx[2 * q + 1]
     live_total = jnp.sum(mvec[...], axis=1, keepdims=True)
 
-    SB = 64
-
-    for view in range(2):
-        def step(ch, acc):
+    SB = 128
+
+    def sq_step(ch, carry):
+        for view in range(2):
             rows, e = exp_block(view, ch)
             a0[view, rows] = e * e
-            return acc + fold(e)
-        acc = lax.fori_loop(0, NCH, step, jnp.zeros((8, NROW), F32))
-        lx[me, view] = jnp.sum(acc, axis=0, keepdims=True)
+        return carry
+    lax.fori_loop(0, NCH, sq_step, 0)
 
     def sink_pass(it):
-        for view in range(2):
-            scale = (1.0 if it == 0 else live_total) * (1.0 / PROTOS)
-
-            def step(blk, acc):
-                rows = pl.ds(pl.multiple_of(blk * SB, SB), SB)
+        scale = (1.0 if it == 0 else live_total) * (1.0 / PROTOS)
+
+        def step(blk, accs):
+            rows = pl.ds(pl.multiple_of(blk * SB, SB), SB)
+            out = []
+            for view in range(2):
                 a = a0[view, rows]
                 w = mvec[...] if it == 0 else wvec[view]
                 colsum = jnp.sum(a * w, axis=1, keepdims=True)
                 v = scale / colsum
                 if it == ITERS - 1:
                     vb[view, rows] = jnp.broadcast_to(v, (SB, 128))
-                return acc + fold(a * v)
-            acc = lax.fori_loop(0, OWN // SB, step, jnp.zeros((8, NROW), F32))
-            rx[it, me, :, view * NROW:(view + 1) * NROW] = jnp.sum(acc, axis=0, keepdims=True)
+                out.append(accs[view] + fold(a * v))
+            return tuple(out)
+        zero = jnp.zeros((8, NROW), F32)
+        accs = lax.fori_loop(0, OWN // SB, step, (zero, zero))
+        for view in range(2):
+            rx[it, me, :, view * NROW:(view + 1) * NROW] = jnp.sum(accs[view], axis=0, keepdims=True)
         bcast(*r_args(it), wait=False)
 
     def sink_close(it):
@@ -232,42 +239,37 @@
 
     sink_pass(0)
     zstart(3)
+    bcast(*l_args, wait=True)
+    grad_scale = 1.0 / (TAU * live_total * (2 + 2 * (VIEWS - 2)))
+    log_sum = jnp.zeros((1, NROW), F32)
+    low = lax.broadcasted_iota(jnp.int32, (1, 128), 1) < ROWS
+    for view in range(VIEWS):
+        tot = jnp.concatenate([jnp.where(low, lx[2 * q, view], lx[2 * q + 1, view])
+                               for q in range(NROW // 128)], axis=1)
+        mult = 1.0 if view < 2 else 2.0
+        acf[view] = (mult * grad_scale) * mvec[...] / tot
+        log_sum = log_sum + mult * jnp.log(tot)
+    log_sum = jnp.sum(log_sum * mvec[...], axis=1, keepdims=True)
     zforward((2,))
-    zfinish((2,))
-    exp_views(2, 6)
-    bcast(*l_args(0), wait=False)
     sink_close(0)
     sink_pass(1)
     zstart(4)
+    zfinish((2,))
+    exp_views(2, 6)
     zforward((3,))
+    sink_close(1)
+    sink_pass(2)
     zfinish((3,))
     exp_views(6, 9)
-    sink_close(1)
-    sink_pass(2)
-    zforward((4,))
-    zfinish((4,))
-    exp_views(9, 12)
-    bcast(*l_args(1), wait=False)
-
     for view in range(2):
         for blk in range(OWN // 128):
             vt = vb[view, blk * 128:(blk + 1) * 128].T
             vx[me, view, :, blk * 128:(blk + 1) * 128] = vt[0:1, :]
     bcast(*v_args, wait=False)
-
+    zforward((4,))
+    zfinish((4,))
+    exp_views(9, 12)
     sink_close(2)
-    bcast(*l_args(0), wait=True)
-    bcast(*l_args(1), wait=True)
-    grad_scale = 1.0 / (TAU * live_total * (2 + 2 * (VIEWS - 2)))
-    log_sum = jnp.zeros((1, NROW), F32)
-    for view in range(VIEWS):
-        tot = lx[0, view]
-        for d in range(1, DEVS):
-            tot = tot + lx[d, view]
-        mult = 1.0 if view < 2 else 2.0
-        acf[view] = (mult * grad_scale) * mvec[...] / tot
-        log_sum = log_sum + mult * jnp.log(tot)
-    log_sum = jnp.sum(log_sum * mvec[...], axis=1, keepdims=True)
 
     def acopy(src_dev, ch, half, to, kind):
         lo = src_dev * OWN + ch * KC
@@ -281,20 +283,16 @@
 
     def dc_chunk(ch, carry):
         rows = pl.ds(pl.multiple_of(ch * KC, KC), KC)
+        gq = []
         for view in range(2):
-            v = vb[view, rows]
-            v = jnp.concatenate([v] * (NROW // 128), axis=1)
-            gq[view] = (wvec[view] * grad_scale) * (v * a0[view, rows])
-        gq[2] = gq[0] + gq[1]
-        g0 = (acf[0] * et[0, rows] - gq[1]).astype(BF16)
-        acc = jnp.dot(g0, zall[0], preferred_element_type=F32)
-        g1 = (acf[1] * et[1, rows] - gq[0]).astype(BF16)
-        acc = acc + jnp.dot(g1, zall[1], preferred_element_type=F32)
-
-        def step(view, acc):
-            g = (acf[view] * et[view, rows] - gq[2]).astype(BF16)
-            return acc + jnp.dot(g, zall[view], preferred_element_type=F32)
-        acc = lax.fori_loop(2, VIEWS, step, acc)
+            v = jnp.concatenate([vb[view, rows]] * (NROW // 128), axis=1)
+            gq.append((wvec[view] * grad_scale) * (v * a0[view, rows]))
+        sub = [gq[1], gq[0]] + [gq[0] + gq[1]] * (VIEWS - 2)
+        acc = None
+        for view in range(VIEWS):
+            g = (acf[view] * et[view, rows] - sub[view]).astype(BF16)
+            part = jnp.dot(g, zall[view], preferred_element_type=F32)
+            acc = part if acc is None else acc + part
         dcv[pl.ds(pl.multiple_of(own0 + ch * KC, KC), KC)] = acc
         for kind, to in ((0, xn), (1, yn), (2, partner)):
             acopy(me, ch, None, to, kind).start()
@@ -311,25 +309,14 @@
     for j in range(VIEWS + 2):
         ab[j] = jnp.broadcast_to(own_cf[:, j:j + 1], (ROWS, 128))
 
-    for copy in c_copies:
-        copy.wait()
     bcast(*v_args, wait=True)
-    dzacc[...] = jnp.zeros_like(dzacc)
+    dz_out[...] = jnp.zeros_like(dz_out)
 
     def wide(x):
         return jnp.concatenate([x] * (PC // 128), axis=1)
 
-    def qcopy(view, ch, slot):
+    def row_chunk(ch, acc):
         cols = pl.ds(pl.multiple_of(ch * PC, PC), PC)
-        return pltpu.make_async_copy(qbuf.at[slot, view], (q1_hbm, q2_hbm)[view].at[:, cols], qsem.at[slot, view])
-
-    def row_chunk(ch, acc):
-        slot = ch % 2
-
-        @pl.when(ch >= 2)
-        def _():
-            for view in range(2):
-                qcopy(view, ch - 2, slot).wait()
         cc = cv[pl.ds(pl.multiple_of(ch * PC, PC), PC)]
         scores = nt_dot(zown[...].reshape(VIEWS * ROWS, DIM), cc)
         dev = ch // (OWN // PC)
@@ -338,7 +325,7 @@
         for view in range(2):
             e = jnp.exp(scores[view * ROWS:(view + 1) * ROWS] * (1.0 / TAU))
             q = wide(ab[VIEWS + view]) * (vx[dev, view, :, half] * (e * e))
-            qbuf[slot, view] = q
+            q_out[view, :, cols] = q
             e_large.append(e)
             q_large.append(q)
         q_sum = q_large[0] + q_large[1]
@@ -351,26 +338,13 @@
             s_sum = s if s_sum is None else s_sum + s
             parts.append((wide(ab[view]) * jnp.exp(s * (1.0 / TAU)) - gq_sum).astype(BF16))
         dot = q_large[1] * scores[0:ROWS] + q_large[0] * scores[ROWS:2 * ROWS] + q_sum * s_sum
-        for view in range(2):
-            qcopy(view, ch, slot).start()
-        dzacc[...] += jnp.dot(jnp.concatenate(parts, axis=0), cc, preferred_element_type=F32)
+        dz = jnp.dot(jnp.concatenate(parts, axis=0), cc, preferred_element_type=F32)
+        dz_out[...] += dz.reshape(VIEWS, ROWS, DIM)
         return acc + fold(dot)
     acc = lax.fori_loop(0, PROTOS // PC, row_chunk, jnp.zeros((8, PC), F32))
     cross = jnp.sum(jnp.sum(acc, axis=0, keepdims=True), axis=1, keepdims=True)
     px[me] = jnp.broadcast_to(cross, (1, 128))
     bcast(*p_args, wait=False)
-    dz1_ref[...] = dzacc[0:ROWS]
-    dz2_ref[...] = dzacc[ROWS:2 * ROWS]
-    for view in range(VIEWS - 2):
-        dzs_ref[view] = dzacc[(view + 2) * ROWS:(view + 3) * ROWS]
-
-    def out_copy(dev, ch, half, kind):
-        lo = dev * OWN + ch * KC
-        if half is None:
-            rows = pl.ds(pl.multiple_of(lo, KC), KC)
-        else:
-            rows = pl.ds(pl.multiple_of(lo + half * (KC // 2), KC // 2), KC // 2)
-        return pltpu.make_async_copy(dcv.at[rows], dc_hbm.at[rows], osem.at[kind, ch])
 
     def gather_near(ch, carry):
         acopy(xn, ch, None, xn, 0).wait_recv()
@@ -379,11 +353,7 @@
         acopy(yn, ch, None, yn, 1).wait_recv()
         acopy(yn, ch, 1, xn, 4).start()
         acopy(yn, ch, None, partner, 6).start()
-        out_copy(me, ch, None, 0).start()
-        out_copy(xn, ch, None, 1).start()
-        out_copy(yn, ch, None, 2).start()
         acopy(partner, ch, None, partner, 2).wait_recv()
-        out_copy(partner, ch, None, 3).start()
         return carry
 
     def gather_far(ch, carry):
@@ -391,14 +361,10 @@
         acopy(dg, ch, 0, partner, 7).start()
         acopy(dg, ch, 1, xn, 4).wait_recv()
         acopy(dg, ch, 1, partner, 8).start()
-        out_copy(dg, ch, None, 4).start()
         acopy(other(xn), ch, None, partner, 5).wait_recv()
-        out_copy(other(xn), ch, None, 5).start()
         acopy(other(yn), ch, None, partner, 6).wait_recv()
-        out_copy(other(yn), ch, None, 6).start()
         acopy(other(dg), ch, 0, partner, 7).wait_recv()
         acopy(other(dg), ch, 1, partner, 8).wait_recv()
-        out_copy(other(dg), ch, None, 7).start()
         return carry
     lax.fori_loop(0, NCH, gather_near, 0)
     bcast(*p_args, wait=True)
@@ -418,8 +384,6 @@
         acopy(yn, ch, None, partner, 6).wait_send()
         acopy(dg, ch, 0, partner, 7).wait_send()
         acopy(dg, ch, 1, partner, 8).wait_send()
-        for kind, dev in enumerate((me, xn, yn, partner, dg, other(xn), other(yn), other(dg))):
-            out_copy(dev, ch, None, kind).wait()
         return carry
     for unit in range(len(UNITS)):
         for kind in range(7):
@@ -429,12 +393,19 @@
     bcast_drain(*v_args)
     for it in range(ITERS):
         bcast_drain(*r_args(it))
-    for part in range(2):
-        bcast_drain(*l_args(part))
-    for ch in (PROTOS // PC - 2, PROTOS // PC - 1):
-        for view in range(2):
-            qcopy(view, ch, ch % 2).wait()
+    bcast_drain(*l_args)
     lax.fori_loop(0, NCH, drain, 0)
+
+
+def write_out(q_ref, loss_in, dz_ref, dc_ref, q1_hbm, q2_hbm, loss_ref, dz1_hbm, dz2_hbm, dzs_hbm, dc_hbm, sem):
+    copies = []
+    for src, dst in ((dc_ref, dc_hbm), (q_ref.at[0], q1_hbm), (q_ref.at[1], q2_hbm),
+                     (dz_ref.at[pl.ds(2, VIEWS - 2)], dzs_hbm), (dz_ref.at[0], dz1_hbm), (dz_ref.at[1], dz2_hbm)):
+        copies.append(pltpu.make_async_copy(src, dst, sem.at[len(copies)]))
+        copies[-1].start()
+    loss_ref[0, 0] = jnp.max(loss_in[:, 0:1])
+    for copy in copies:
+        copy.wait()
 
 
 def local_step(z_one, z_two, z_small, protos, live_mask):
@@ -442,33 +413,26 @@
     hbm = pl.BlockSpec(memory_space=pl.ANY)
     dma = pltpu.SemaphoreType.DMA
     views = VIEWS
-    out = pl.pallas_call(
+    staged = pl.pallas_call(
         body,
         out_shape=(
-            jax.ShapeDtypeStruct((ROWS, PROTOS), F32),
-            jax.ShapeDtypeStruct((ROWS, PROTOS), F32),
-            jax.ShapeDtypeStruct((1, 128), F32),
-            jax.ShapeDtypeStruct((ROWS, DIM), F32),
-            jax.ShapeDtypeStruct((ROWS, DIM), F32),
-            jax.ShapeDtypeStruct((views - 2, ROWS, DIM), F32),
-            jax.ShapeDtypeStruct((PROTOS, DIM), F32),
+            pltpu.VMEM((2, ROWS, PROTOS), F32),
+            pltpu.VMEM((1, 128), F32),
+            pltpu.VMEM((views, ROWS, DIM), F32),
+            pltpu.VMEM((PROTOS, DIM), F32),
         ),
         in_specs=[vmem, vmem, vmem, vmem, hbm],
-        out_specs=(hbm, hbm, vmem, vmem, vmem, vmem, hbm),
+        out_specs=(vmem, vmem, vmem, vmem),
         scratch_shapes=[
             pltpu.VMEM((views, NROW, DIM), BF16),
             pltpu.VMEM((views, ROWS, DIM), BF16),
             pltpu.VMEM((PROTOS, DIM), BF16),
             pltpu.VMEM((views, OWN, NROW), F32),
             pltpu.VMEM((2, OWN, NROW), F32),
-            pltpu.VMEM((3, KC, NROW), F32),
-            pltpu.VMEM((8, 128), BF16),
-            pltpu.VMEM((PROTOS, DIM), F32),
-            pltpu.VMEM((2, 2, ROWS, PC), F32),
             pltpu.VMEM((2, OWN, 128), F32),
             pltpu.VMEM((DEVS, 2, 1, OWN), F32),
             pltpu.VMEM((ITERS, DEVS, 1, 2 * NROW), F32),
-            pltpu.VMEM((DEVS, views, 1, NROW), F32),
+            pltpu.VMEM((DEVS, views, 1, 128), F32),
             pltpu.VMEM((DEVS, 1, 128), F32),
             pltpu.VMEM((DEVS, 1, 128), F32),
             pltpu.VMEM((1, NROW), F32),
@@ -477,23 +441,36 @@
             pltpu.VMEM((128, 128), F32),
             pltpu.VMEM((128, 128), F32),
             pltpu.VMEM((views + 2, ROWS, 128), F32),
-            pltpu.VMEM((8, 128), F32),
-            pltpu.VMEM((views * ROWS, DIM), F32),
-            dma((DEVS,)),
+            pltpu.VMEM((views * ROWS, 128), F32),
+            dma(()),
             dma((7, 5)), dma((7, 5)),
             dma((ITERS, DEVS)), dma((ITERS, DEVS)),
-            dma((2, DEVS)), dma((2, DEVS)),
+            dma((DEVS,)), dma((DEVS,)),
             dma((DEVS,)), dma((DEVS,)),
             dma((2, DEVS)), dma((2, DEVS)),
             dma((9, NCH)), dma((9, NCH)),
-            dma((2, 2)),
-            dma((8, NCH)),
         ],
         compiler_params=pltpu.CompilerParams(
-            collective_id=0, has_side_effects=True, vmem_limit_bytes=62 * 1024 * 1024),
+            collective_id=0, has_side_effects=True, vmem_limit_bytes=48 * 1024 * 1024),
         name="swav_step",
     )(live_mask.reshape(1, ROWS), z_one, z_two, z_small, protos)
-    q_one, q_two, loss, dz_one, dz_two, dz_small, d_protos = out
+    q_one, q_two, loss, dz_one, dz_two, dz_small, d_protos = pl.pallas_call(
+        write_out,
+        out_shape=(
+            jax.ShapeDtypeStruct((ROWS, PROTOS), F32),
+            jax.ShapeDtypeStruct((ROWS, PROTOS), F32),
+            jax.ShapeDtypeStruct((1, 1), F32),
+            jax.ShapeDtypeStruct((ROWS, DIM), F32),
+            jax.ShapeDtypeStruct((ROWS, DIM), F32),
+            jax.ShapeDtypeStruct((views - 2, ROWS, DIM), F32),
+            jax.ShapeDtypeStruct((PROTOS, DIM), F32),
+        ),
+        in_specs=[vmem] * 4,
+        out_specs=(hbm, hbm, pl.BlockSpec(memory_space=pltpu.SMEM), hbm, hbm, hbm, hbm),
+        scratch_shapes=[dma((6,))],
+        compiler_params=pltpu.CompilerParams(vmem_limit_bytes=1024 * 1024),
+        name="write_out",
+    )(*staged)
     return q_one, q_two, loss[0, 0], dz_one, dz_two, dz_small, d_protos
 
 

time: 103 us -> 80.7 us (0.78)
  local copies, waits for them, and re-layouts: 14 us -> 0 us
  Pallas kernels: 86.7 us -> 79.9 us
  between operations: 1.85 us -> 0.64 us
    unnamed x16 -> x0, local copies, waits for them, and re-layouts: 14 us -> none
    pallas_call x1 -> x2, Pallas kernels: 86.7 us -> 79.9 us  [the longest x1 74.4 us: local_step(): pl.pallas_call(body, out_shape=(pltpu.VMEM((2, ROWS, PROTOS), F32), pltpu...]
where the time goes in v2:
time: 80.7 us; the launch traced here: 80.5 us
  Pallas kernels  79.9 us (99%)
    pallas_call x1, Pallas kernels, local_step(): pl.pallas_call(body, out_shape=(pltpu.VMEM((2, ROWS, PROTOS), F32), pltpu...  74.4 us
    pallas_call x1, Pallas kernels, local_step(): pl.pallas_call(write_out, out_shape=(jax.ShapeDtypeStruct((ROWS, PROTOS),...  5.44 us

profile of v2, /device:TPU:0, one launch (start us, length us, event | category | flops | bytes accessed | tf_op | source)
XLA Modules:
  0.0 80.5 jit_solution(12538176114879877897)
XLA Ops:
  0.6 74.4 %swav_step.1 = (f32[2,64,8192]{2,1,0:T(8,128)S(1)}, f32[1,128]{1,0:T(1,128)S(1)}, f32[12,64,256]{2,1,0:T(8,128)S(1)}, f32[8192,256]{1,0:T(8,128)S(1)}) custom-call(s32[1,64]{1,0:T(1,128)} %bitcast.2, bf16[64,256]{1,0:T(8,128)(2,1)} %z1_ref.1, bf16[64,256]{1,0:T(8,128)(2,1)} %z2_ref.1, bf16[10,64,256]{2,1,0:T(8,128)(2,1)} %zs_ref.1, bf16[8192,256]{1,0:T(8,128)(2,1)} %c_hbm.1), custom_call_target="tpu_custom_call" | custom-call | tf_op jit(solution)/shard_map/swav_step/pallas_call | solution.py:416
  75.1 5.4 %write_out.1 = (f32[64,8192]{1,0:T(8,128)}, f32[64,8192]{1,0:T(8,128)}, f32[1,1]{1,0:T(1,128)}, f32[64,256]{1,0:T(8,128)}, f32[64,256]{1,0:T(8,128)}, /*index=5*/f32[10,64,256]{2,1,0:T(8,128)}, f32[8192,256]{1,0:T(8,128)}) custom-call(f32[2,64,8192]{2,1,0:T(8,128)S(1)} %get-tuple-element.18.q_ref, f32[1,128]{1,0:T(1,128)S(1)} %get-tuple-element.19.loss_in, ...), custom_call_target="tpu_custom_call" | custom-call | tf_op jit(solution)/shard_map/write_out/pallas_call | solution.py:457

commit v3 on v2

--- a/solution.py
+++ b/solution.py
@@ -24,7 +24,9 @@
 MESH = pl.DeviceIdType.MESH
 F32 = jnp.float32
 BF16 = jnp.bfloat16
-UNITS = ((0, 1), (1, 1), (2, 4), (6, 3), (9, 3))
+UNITS = ((0, 1), (1, 1), (2, 4), (6, 4), (10, 2))
+SENT = 2
+EC = 512
 
 
 def nt_dot(a, b):
@@ -173,26 +175,29 @@
         scores = nt_dot(zown[...].reshape(VIEWS * ROWS, DIM), cc)
         lacc[...] += lane_fold(jnp.exp(scores * (1.0 / TAU)))
         return carry
-    lax.fori_loop(0, PROTOS // PC, sum_chunk, 0)
-    for view in range(VIEWS):
-        la = lacc[view * ROWS:(view + 1) * ROWS]
-        lx[me, view] = jnp.sum(jnp.concatenate([la, la], axis=0).T, axis=0, keepdims=True)
-    bcast(*l_args, wait=False)
+    def row_sums_out():
+        for view in range(VIEWS):
+            la = lacc[view * ROWS:(view + 1) * ROWS]
+            lx[me, view] = jnp.sum(jnp.concatenate([la, la], axis=0).T, axis=0, keepdims=True)
+        bcast(*l_args, wait=False)
 
     def exp_block(view, ch):
-        rows = pl.ds(pl.multiple_of(ch * KC, KC), KC)
-        scores = nt_dot(cv[pl.ds(pl.multiple_of(own0 + ch * KC, KC), KC)], zall[view])
+        rows = pl.ds(pl.multiple_of(ch * EC, EC), EC)
+        scores = nt_dot(cv[pl.ds(pl.multiple_of(own0 + ch * EC, EC), EC)], zall[view])
         e = jnp.exp(scores * (1.0 / TAU))
         et[view, rows] = e
         return rows, e
 
     def exp_views(lo, hi):
-        def step(i, carry):
-            exp_block(lo + i // NCH, i % NCH)
+        def step(view, carry):
+            for ch in range(OWN // EC):
+                exp_block(view, ch)
             return carry
-        lax.fori_loop(0, (hi - lo) * NCH, step, 0)
-
+        lax.fori_loop(lo, hi, step, 0)
+
+    lax.fori_loop(0, 6, sum_chunk, 0)
     zforward((0, 1))
+    lax.fori_loop(6, 8, sum_chunk, 0)
     bcast(*m_args, wait=True)
     zfinish((0, 1))
     for q in range(NROW // 128):
@@ -201,12 +206,11 @@
 
     SB = 128
 
-    def sq_step(ch, carry):
-        for view in range(2):
-            rows, e = exp_block(view, ch)
-            a0[view, rows] = e * e
-        return carry
-    lax.fori_loop(0, NCH, sq_step, 0)
+    def sq_step(i, carry):
+        rows, e = exp_block(i // 2, i % 2)
+        a0[i // 2, rows] = e * e
+        return carry
+    lax.fori_loop(0, 2 * (OWN // EC), sq_step, 0)
 
     def sink_pass(it):
         scale = (1.0 if it == 0 else live_total) * (1.0 / PROTOS)
@@ -239,6 +243,17 @@
 
     sink_pass(0)
     zstart(3)
+    lax.fori_loop(8, PROTOS // PC, sum_chunk, 0)
+    row_sums_out()
+    zforward((2,))
+    sink_close(0)
+    sink_pass(1)
+    zstart(4)
+    zfinish((2,))
+    exp_views(2, 6)
+    zforward((3,))
+    sink_close(1)
+    sink_pass(2)
     bcast(*l_args, wait=True)
     grad_scale = 1.0 / (TAU * live_total * (2 + 2 * (VIEWS - 2)))
     log_sum = jnp.zeros((1, NROW), F32)
@@ -250,25 +265,16 @@
         acf[view] = (mult * grad_scale) * mvec[...] / tot
         log_sum = log_sum + mult * jnp.log(tot)
     log_sum = jnp.sum(log_sum * mvec[...], axis=1, keepdims=True)
-    zforward((2,))
-    sink_close(0)
-    sink_pass(1)
-    zstart(4)
-    zfinish((2,))
-    exp_views(2, 6)
-    zforward((3,))
-    sink_close(1)
-    sink_pass(2)
-    zfinish((3,))
-    exp_views(6, 9)
     for view in range(2):
         for blk in range(OWN // 128):
             vt = vb[view, blk * 128:(blk + 1) * 128].T
             vx[me, view, :, blk * 128:(blk + 1) * 128] = vt[0:1, :]
     bcast(*v_args, wait=False)
+    zfinish((3,))
+    exp_views(6, 10)
     zforward((4,))
     zfinish((4,))
-    exp_views(9, 12)
+    exp_views(10, 12)
     sink_close(2)
 
     def acopy(src_dev, ch, half, to, kind):
@@ -294,10 +300,59 @@
             part = jnp.dot(g, zall[view], preferred_element_type=F32)
             acc = part if acc is None else acc + part
         dcv[pl.ds(pl.multiple_of(own0 + ch * KC, KC), KC)] = acc
-        for kind, to in ((0, xn), (1, yn), (2, partner)):
-            acopy(me, ch, None, to, kind).start()
-        return carry
-    lax.fori_loop(0, NCH, dc_chunk, 0)
+        acopy(me, ch, None, partner, 2).start()
+        return carry
+
+    def dc_sent(ch, carry):
+        dc_chunk(ch, carry)
+        acopy(me, ch, None, xn, 0).start()
+        acopy(me, ch, None, yn, 1).start()
+        return carry
+    lax.fori_loop(0, SENT, dc_sent, 0)
+    lax.fori_loop(SENT, NCH, dc_chunk, 0)
+
+    def dc_again(i, carry):
+        which = i % 3
+        ch = SENT + i // 3
+        dev = me + (1 - which % 2) * (2 - 4 * xpos) + ((which + 1) // 2) * (4 - 8 * ypos)
+        lo = pl.multiple_of(dev * OWN + ch * KC, KC)
+        cc = cv[pl.ds(lo, KC)]
+
+        def expo(view):
+            return jnp.exp(nt_dot(cc, zall[view]) * (1.0 / TAU))
+        gq, es = [], []
+        for view in range(2):
+            vrow = vx[dev, view, :, pl.ds(pl.multiple_of(ch * KC, KC), KC)]
+            v = jnp.concatenate([jnp.broadcast_to(vrow[:, j * 128:(j + 1) * 128], (128, 128)).T
+                                 for j in range(KC // 128)], axis=0)
+            v = jnp.concatenate([v] * (NROW // 128), axis=1)
+            e = expo(view)
+            es.append(e)
+            gq.append((wvec[view] * grad_scale) * (v * (e * e)))
+        sub = [gq[1], gq[0]] + [gq[0] + gq[1]] * (VIEWS - 2)
+        acc = None
+        for view in range(VIEWS):
+            e = es[view] if view < 2 else expo(view)
+            g = (acf[view] * e - sub[view]).astype(BF16)
+            part = jnp.dot(g, zall[view], preferred_element_type=F32)
+            acc = part if acc is None else acc + part
+        dcv[pl.ds(lo, KC)] = acc
+        acopy(dev, ch, None, partner, 5 + which).start()
+        return carry
+
+    def relay(ch):
+        acopy(xn, ch, None, xn, 0).wait_recv()
+        acopy(xn, ch, 0, yn, 3).start()
+        acopy(xn, ch, None, partner, 5).start()
+        acopy(yn, ch, None, yn, 1).wait_recv()
+        acopy(yn, ch, 1, xn, 4).start()
+        acopy(yn, ch, None, partner, 6).start()
+
+    bcast(*v_args, wait=True)
+    lax.fori_loop(0, 3, dc_again, 0)
+    relay(0)
+    lax.fori_loop(3, 3 * (NCH - SENT), dc_again, 0)
+    relay(1)
 
     lanes = pl.ds(pl.multiple_of((me // 2) * 128, 128), 128)
     for view in range(VIEWS):
@@ -309,7 +364,6 @@
     for j in range(VIEWS + 2):
         ab[j] = jnp.broadcast_to(own_cf[:, j:j + 1], (ROWS, 128))
 
-    bcast(*v_args, wait=True)
     dz_out[...] = jnp.zeros_like(dz_out)
 
     def wide(x):
@@ -346,44 +400,44 @@
     px[me] = jnp.broadcast_to(cross, (1, 128))
     bcast(*p_args, wait=False)
 
-    def gather_near(ch, carry):
-        acopy(xn, ch, None, xn, 0).wait_recv()
-        acopy(xn, ch, 0, yn, 3).start()
-        acopy(xn, ch, None, partner, 5).start()
-        acopy(yn, ch, None, yn, 1).wait_recv()
-        acopy(yn, ch, 1, xn, 4).start()
-        acopy(yn, ch, None, partner, 6).start()
-        acopy(partner, ch, None, partner, 2).wait_recv()
-        return carry
-
     def gather_far(ch, carry):
         acopy(dg, ch, 0, yn, 3).wait_recv()
         acopy(dg, ch, 0, partner, 7).start()
         acopy(dg, ch, 1, xn, 4).wait_recv()
         acopy(dg, ch, 1, partner, 8).start()
-        acopy(other(xn), ch, None, partner, 5).wait_recv()
-        acopy(other(yn), ch, None, partner, 6).wait_recv()
-        acopy(other(dg), ch, 0, partner, 7).wait_recv()
-        acopy(other(dg), ch, 1, partner, 8).wait_recv()
-        return carry
-    lax.fori_loop(0, NCH, gather_near, 0)
+        return carry
+
     bcast(*p_args, wait=True)
     tot = px[0]
     for d in range(1, DEVS):
         tot = tot + px[d]
     loss = -(tot[:, 0:1] * (1.0 / TAU) - log_sum) / (live_total * (2 + 2 * (VIEWS - 2)))
     loss_ref[...] = jnp.broadcast_to(loss, (1, 128))
-    lax.fori_loop(0, NCH, gather_far, 0)
-
-    def drain(ch, carry):
-        for kind in (0, 1, 2):
+    lax.fori_loop(0, SENT, gather_far, 0)
+
+    def drain_sent(ch, carry):
+        acopy(other(dg), ch, 0, partner, 7).wait_recv()
+        acopy(other(dg), ch, 1, partner, 8).wait_recv()
+        for kind in (0, 1):
             acopy(me, ch, None, partner, kind).wait_send()
         acopy(xn, ch, 0, yn, 3).wait_send()
         acopy(yn, ch, 1, xn, 4).wait_send()
+        acopy(dg, ch, 0, partner, 7).wait_send()
+        acopy(dg, ch, 1, partner, 8).wait_send()
+        return carry
+
+    def drain_again(ch, carry):
+        acopy(other(dg), ch, None, partner, 7).wait_recv()
+        acopy(dg, ch, None, partner, 7).wait_send()
+        return carry
+
+    def drain(ch, carry):
+        acopy(partner, ch, None, partner, 2).wait_recv()
+        acopy(other(xn), ch, None, partner, 5).wait_recv()
+        acopy(other(yn), ch, None, partner, 6).wait_recv()
+        acopy(me, ch, None, partner, 2).wait_send()
         acopy(xn, ch, None, partner, 5).wait_send()
         acopy(yn, ch, None, partner, 6).wait_send()
-        acopy(dg, ch, 0, partner, 7).wait_send()
-        acopy(dg, ch, 1, partner, 8).wait_send()
         return carry
     for unit in range(len(UNITS)):
         for kind in range(7):
@@ -395,6 +449,8 @@
         bcast_drain(*r_args(it))
     bcast_drain(*l_args)
     lax.fori_loop(0, NCH, drain, 0)
+    lax.fori_loop(SENT, NCH, drain_again, 0)
+    lax.fori_loop(0, SENT, drain_sent, 0)
 
 
 def write_out(q_ref, loss_in, dz_ref, dc_ref, q1_hbm, q2_hbm, loss_ref, dz1_hbm, dz2_hbm, dzs_hbm, dc_hbm, sem):

time: 80.7 us -> 72.2 us (0.89)
  Pallas kernels: 79.9 us -> 71.4 us
    pallas_call x1, Pallas kernels: 74.4 us -> 66 us  [local_step(): pl.pallas_call(body, out_shape=(pltpu.VMEM((2, ROWS, PROTOS), F32), pltpu...]
where the time goes in v3:
time: 72.2 us; the launch traced here: 72.1 us
  Pallas kernels  71.4 us (99%)
    pallas_call x1, Pallas kernels, local_step(): pl.pallas_call(body, out_shape=(pltpu.VMEM((2, ROWS, PROTOS), F32), pltpu...  66 us
    pallas_call x1, Pallas kernels, local_step(): pl.pallas_call(write_out, out_shape=(jax.ShapeDtypeStruct((ROWS, PROTOS),...  5.44 us

profile of v3, /device:TPU:0, one launch (start us, length us, event | category | flops | bytes accessed | tf_op | source)
XLA Modules:
  0.0 72.1 jit_solution(10216641853352596109)
XLA Ops:
  0.6 66.0 %swav_step.1 = (f32[2,64,8192]{2,1,0:T(8,128)S(1)}, f32[1,128]{1,0:T(1,128)S(1)}, f32[12,64,256]{2,1,0:T(8,128)S(1)}, f32[8192,256]{1,0:T(8,128)S(1)}) custom-call(s32[1,64]{1,0:T(1,128)} %bitcast.2, bf16[64,256]{1,0:T(8,128)(2,1)} %z1_ref.1, bf16[64,256]{1,0:T(8,128)(2,1)} %z2_ref.1, bf16[10,64,256]{2,1,0:T(8,128)(2,1)} %zs_ref.1, bf16[8192,256]{1,0:T(8,128)(2,1)} %c_hbm.1), custom_call_target="tpu_custom_call" | custom-call | tf_op jit(solution)/shard_map/swav_step/pallas_call | solution.py:472
  66.6 5.4 %write_out.1 = (f32[64,8192]{1,0:T(8,128)}, f32[64,8192]{1,0:T(8,128)}, f32[1,1]{1,0:T(1,128)}, f32[64,256]{1,0:T(8,128)}, f32[64,256]{1,0:T(8,128)}, /*index=5*/f32[10,64,256]{2,1,0:T(8,128)}, f32[8192,256]{1,0:T(8,128)}) custom-call(f32[2,64,8192]{2,1,0:T(8,128)S(1)} %get-tuple-element.18.q_ref, f32[1,128]{1,0:T(1,128)S(1)} %get-tuple-element.19.loss_in, ...), custom_call_target="tpu_custom_call" | custom-call | tf_op jit(solution)/shard_map/write_out/pallas_call | solution.py:513

commit v4 on v3

--- a/solution.py
+++ b/solution.py
@@ -157,6 +157,8 @@
     zstart(1)
     bcast(*m_args, wait=False)
     zstart(2)
+    zstart(3)
+    zstart(4)
 
     def fold(x):
         return jnp.sum(x.reshape(x.shape[0] // 8, 8, x.shape[1]), axis=0)
@@ -242,13 +244,11 @@
             wvec[view] = mvec[...] / tot[:, view * NROW:(view + 1) * NROW]
 
     sink_pass(0)
-    zstart(3)
     lax.fori_loop(8, PROTOS // PC, sum_chunk, 0)
     row_sums_out()
     zforward((2,))
     sink_close(0)
     sink_pass(1)
-    zstart(4)
     zfinish((2,))
     exp_views(2, 6)
     zforward((3,))

time: 72.2 us -> 77.6 us (1.075)
  Pallas kernels: 71.4 us -> 76.8 us
    pallas_call x1, Pallas kernels: 66 us -> 71.4 us  [local_step(): pl.pallas_call(body, out_shape=(pltpu.VMEM((2, ROWS, PROTOS), F32), pltpu...]
where the time goes in v4:
time: 77.6 us; the launch traced here: 77.5 us
  Pallas kernels  76.8 us (99%)
    pallas_call x1, Pallas kernels, local_step(): pl.pallas_call(body, out_shape=(pltpu.VMEM((2, ROWS, PROTOS), F32), pltpu...  71.4 us
    pallas_call x1, Pallas kernels, local_step(): pl.pallas_call(write_out, out_shape=(jax.ShapeDtypeStruct((ROWS, PROTOS),...  5.44 us

profile of v4, /device:TPU:0, one launch (start us, length us, event | category | flops | bytes accessed | tf_op | source)
XLA Modules:
  0.0 77.5 jit_solution(1812216486960579641)
XLA Ops:
  0.6 71.4 %swav_step.1 = (f32[2,64,8192]{2,1,0:T(8,128)S(1)}, f32[1,128]{1,0:T(1,128)S(1)}, f32[12,64,256]{2,1,0:T(8,128)S(1)}, f32[8192,256]{1,0:T(8,128)S(1)}) custom-call(s32[1,64]{1,0:T(1,128)} %bitcast.2, bf16[64,256]{1,0:T(8,128)(2,1)} %z1_ref.1, bf16[64,256]{1,0:T(8,128)(2,1)} %z2_ref.1, bf16[10,64,256]{2,1,0:T(8,128)(2,1)} %zs_ref.1, bf16[8192,256]{1,0:T(8,128)(2,1)} %c_hbm.1), custom_call_target="tpu_custom_call" | custom-call | tf_op jit(solution)/shard_map/swav_step/pallas_call | solution.py:472
  72.0 5.4 %write_out.1 = (f32[64,8192]{1,0:T(8,128)}, f32[64,8192]{1,0:T(8,128)}, f32[1,1]{1,0:T(1,128)}, f32[64,256]{1,0:T(8,128)}, f32[64,256]{1,0:T(8,128)}, /*index=5*/f32[10,64,256]{2,1,0:T(8,128)}, f32[8192,256]{1,0:T(8,128)}) custom-call(f32[2,64,8192]{2,1,0:T(8,128)S(1)} %get-tuple-element.18.q_ref, f32[1,128]{1,0:T(1,128)S(1)} %get-tuple-element.19.loss_in, ...), custom_call_target="tpu_custom_call" | custom-call | tf_op jit(solution)/shard_map/write_out/pallas_call | solution.py:513

commit v5 on v3

--- a/solution.py
+++ b/solution.py
@@ -25,7 +25,7 @@
 F32 = jnp.float32
 BF16 = jnp.bfloat16
 UNITS = ((0, 1), (1, 1), (2, 4), (6, 4), (10, 2))
-SENT = 2
+SENT = 3
 EC = 512
 
 
@@ -349,10 +349,8 @@
         acopy(yn, ch, None, partner, 6).start()
 
     bcast(*v_args, wait=True)
-    lax.fori_loop(0, 3, dc_again, 0)
+    lax.fori_loop(0, 3 * (NCH - SENT), dc_again, 0)
     relay(0)
-    lax.fori_loop(3, 3 * (NCH - SENT), dc_again, 0)
-    relay(1)
 
     lanes = pl.ds(pl.multiple_of((me // 2) * 128, 128), 128)
     for view in range(VIEWS):
@@ -395,7 +393,10 @@
         dz = jnp.dot(jnp.concatenate(parts, axis=0), cc, preferred_element_type=F32)
         dz_out[...] += dz.reshape(VIEWS, ROWS, DIM)
         return acc + fold(dot)
-    acc = lax.fori_loop(0, PROTOS // PC, row_chunk, jnp.zeros((8, PC), F32))
+    acc = lax.fori_loop(0, PROTOS // PC // 2, row_chunk, jnp.zeros((8, PC), F32))
+    relay(1)
+    acc = lax.fori_loop(PROTOS // PC // 2, PROTOS // PC, row_chunk, acc)
+    relay(2)
     cross = jnp.sum(jnp.sum(acc, axis=0, keepdims=True), axis=1, keepdims=True)
     px[me] = jnp.broadcast_to(cross, (1, 128))
     bcast(*p_args, wait=False)

time: 72.2 us -> 68.6 us (0.950)
  Pallas kernels: 71.4 us -> 67.8 us
    pallas_call x1, Pallas kernels: 66 us -> 62.4 us  [local_step(): pl.pallas_call(body, out_shape=(pltpu.VMEM((2, ROWS, PROTOS), F32), pltpu...]
where the time goes in v5:
time: 68.6 us; the launch traced here: 68.5 us
  Pallas kernels  67.8 us (99%)
    pallas_call x1, Pallas kernels, local_step(): pl.pallas_call(body, out_shape=(pltpu.VMEM((2, ROWS, PROTOS), F32), pltpu...  62.4 us
    pallas_call x1, Pallas kernels, local_step(): pl.pallas_call(write_out, out_shape=(jax.ShapeDtypeStruct((ROWS, PROTOS),...  5.44 us

profile of v5, /device:TPU:0, one launch (start us, length us, event | category | flops | bytes accessed | tf_op | source)
XLA Modules:
  0.0 68.5 jit_solution(11420735498377661744)
XLA Ops:
  0.6 62.4 %swav_step.1 = (f32[2,64,8192]{2,1,0:T(8,128)S(1)}, f32[1,128]{1,0:T(1,128)S(1)}, f32[12,64,256]{2,1,0:T(8,128)S(1)}, f32[8192,256]{1,0:T(8,128)S(1)}) custom-call(s32[1,64]{1,0:T(1,128)} %bitcast.2, bf16[64,256]{1,0:T(8,128)(2,1)} %z1_ref.1, bf16[64,256]{1,0:T(8,128)(2,1)} %z2_ref.1, bf16[10,64,256]{2,1,0:T(8,128)(2,1)} %zs_ref.1, bf16[8192,256]{1,0:T(8,128)(2,1)} %c_hbm.1), custom_call_target="tpu_custom_call" | custom-call | tf_op jit(solution)/shard_map/swav_step/pallas_call | solution.py:473
  63.1 5.4 %write_out.1 = (f32[64,8192]{1,0:T(8,128)}, f32[64,8192]{1,0:T(8,128)}, f32[1,1]{1,0:T(1,128)}, f32[64,256]{1,0:T(8,128)}, f32[64,256]{1,0:T(8,128)}, /*index=5*/f32[10,64,256]{2,1,0:T(8,128)}, f32[8192,256]{1,0:T(8,128)}) custom-call(f32[2,64,8192]{2,1,0:T(8,128)S(1)} %get-tuple-element.18.q_ref, f32[1,128]{1,0:T(1,128)S(1)} %get-tuple-element.19.loss_in, ...), custom_call_target="tpu_custom_call" | custom-call | tf_op jit(solution)/shard_map/write_out/pallas_call | solution.py:514

commit v6 on v3

--- a/solution.py
+++ b/solution.py
@@ -25,7 +25,7 @@
 F32 = jnp.float32
 BF16 = jnp.bfloat16
 UNITS = ((0, 1), (1, 1), (2, 4), (6, 4), (10, 2))
-SENT = 2
+SENT = 3
 EC = 512
 
 
@@ -33,11 +33,11 @@
     return lax.dot_general(a, b, (((1,), (1,)), ((), ())), preferred_element_type=F32)
 
 
-def body(mask_ref, z1_ref, z2_ref, zs_ref, c_hbm,
+def body(mask_ref, z1_hbm, z2_hbm, zs_hbm, c_hbm,
          q_out, loss_ref, dz_out, dcv,
          zall, zown, cv, et, a0, vb, vx, rx, lx, mx, px,
          mvec, wvec, acf, cf, ct, ab, lacc,
-         csem, zsend, zrecv, rsend, rrecv, lsend, lrecv, vsend, vrecv, psend, precv,
+         csem, isem, zsend, zrecv, rsend, rrecv, lsend, lrecv, vsend, vrecv, psend, precv,
          asend, arecv):
     me = lax.axis_index("data")
     core = me % 2
@@ -51,6 +51,13 @@
     def other(d):
         return d + 1 - 2 * core
 
+    my_rows = pl.ds(pl.multiple_of(me * ROWS, ROWS), ROWS)
+    small = pl.ds(2, VIEWS - 2)
+    own_copies = []
+    for src, dst in ((z1_hbm, zown.at[0]), (z2_hbm, zown.at[1]), (zs_hbm, zown.at[small]),
+                     (z1_hbm, zall.at[0, my_rows]), (z2_hbm, zall.at[1, my_rows]), (zs_hbm, zall.at[small, my_rows])):
+        own_copies.append(pltpu.make_async_copy(src, dst, isem.at[len(own_copies)]))
+        own_copies[-1].start()
     own0 = pl.multiple_of(me * OWN, OWN)
     c_copy = pltpu.make_async_copy(c_hbm, cv, csem)
     c_copy.start()
@@ -75,11 +82,7 @@
 
     def zsrc(unit):
         lo, cnt = UNITS[unit]
-        if unit == 0:
-            return z1_ref
-        if unit == 1:
-            return z2_ref
-        return zs_ref.at[pl.ds(lo - 2, cnt)]
+        return zown.at[lo] if cnt == 1 else zown.at[pl.ds(lo, cnt)]
 
     peers = (partner, xn, yn, dg)
 
@@ -143,15 +146,8 @@
 
     l_args = (lambda d: lx.at[d], lambda o: lsend.at[o], lambda d: lrecv.at[d])
 
-    my_rows = pl.ds(pl.multiple_of(me * ROWS, ROWS), ROWS)
-    zall[0, my_rows] = z1_ref[...]
-    zall[1, my_rows] = z2_ref[...]
-    zown[0] = z1_ref[...]
-    zown[1] = z2_ref[...]
-    for view in range(VIEWS - 2):
-        zall[2 + view, my_rows] = zs_ref[view]
-        zown[2 + view] = zs_ref[view]
-
+    for copy in own_copies:
+        copy.wait()
     pl.semaphore_wait(barrier, DEVS - 1)
     zstart(0)
     zstart(1)
@@ -349,9 +345,9 @@
         acopy(yn, ch, None, partner, 6).start()
 
     bcast(*v_args, wait=True)
-    lax.fori_loop(0, 3, dc_again, 0)
+    lax.fori_loop(0, 2, dc_again, 0)
     relay(0)
-    lax.fori_loop(3, 3 * (NCH - SENT), dc_again, 0)
+    lax.fori_loop(2, 3, dc_again, 0)
     relay(1)
 
     lanes = pl.ds(pl.multiple_of((me // 2) * 128, 128), 128)
@@ -395,17 +391,21 @@
         dz = jnp.dot(jnp.concatenate(parts, axis=0), cc, preferred_element_type=F32)
         dz_out[...] += dz.reshape(VIEWS, ROWS, DIM)
         return acc + fold(dot)
-    acc = lax.fori_loop(0, PROTOS // PC, row_chunk, jnp.zeros((8, PC), F32))
-    cross = jnp.sum(jnp.sum(acc, axis=0, keepdims=True), axis=1, keepdims=True)
-    px[me] = jnp.broadcast_to(cross, (1, 128))
-    bcast(*p_args, wait=False)
-
-    def gather_far(ch, carry):
+    def far(ch):
         acopy(dg, ch, 0, yn, 3).wait_recv()
         acopy(dg, ch, 0, partner, 7).start()
         acopy(dg, ch, 1, xn, 4).wait_recv()
         acopy(dg, ch, 1, partner, 8).start()
-        return carry
+
+    acc = lax.fori_loop(0, 6, row_chunk, jnp.zeros((8, PC), F32))
+    relay(2)
+    acc = lax.fori_loop(6, 12, row_chunk, acc)
+    far(0)
+    far(1)
+    acc = lax.fori_loop(12, PROTOS // PC, row_chunk, acc)
+    cross = jnp.sum(jnp.sum(acc, axis=0, keepdims=True), axis=1, keepdims=True)
+    px[me] = jnp.broadcast_to(cross, (1, 128))
+    bcast(*p_args, wait=False)
 
     bcast(*p_args, wait=True)
     tot = px[0]
@@ -413,7 +413,7 @@
         tot = tot + px[d]
     loss = -(tot[:, 0:1] * (1.0 / TAU) - log_sum) / (live_total * (2 + 2 * (VIEWS - 2)))
     loss_ref[...] = jnp.broadcast_to(loss, (1, 128))
-    lax.fori_loop(0, SENT, gather_far, 0)
+    far(2)
 
     def drain_sent(ch, carry):
         acopy(other(dg), ch, 0, partner, 7).wait_recv()
@@ -455,8 +455,16 @@
 
 def write_out(q_ref, loss_in, dz_ref, dc_ref, q1_hbm, q2_hbm, loss_ref, dz1_hbm, dz2_hbm, dzs_hbm, dc_hbm, sem):
     copies = []
-    for src, dst in ((dc_ref, dc_hbm), (q_ref.at[0], q1_hbm), (q_ref.at[1], q2_hbm),
-                     (dz_ref.at[pl.ds(2, VIEWS - 2)], dzs_hbm), (dz_ref.at[0], dz1_hbm), (dz_ref.at[1], dz2_hbm)):
+    pairs = []
+    for i in range(8):
+        rows = pl.ds(i * (PROTOS // 8), PROTOS // 8)
+        pairs.append((dc_ref.at[rows], dc_hbm.at[rows]))
+    for i in range(4):
+        rows = pl.ds(i * (ROWS // 4), ROWS // 4)
+        pairs.append((q_ref.at[0, rows], q1_hbm.at[rows]))
+        pairs.append((q_ref.at[1, rows], q2_hbm.at[rows]))
+    pairs += [(dz_ref.at[pl.ds(2, VIEWS - 2)], dzs_hbm), (dz_ref.at[0], dz1_hbm), (dz_ref.at[1], dz2_hbm)]
+    for src, dst in pairs:
         copies.append(pltpu.make_async_copy(src, dst, sem.at[len(copies)]))
         copies[-1].start()
     loss_ref[0, 0] = jnp.max(loss_in[:, 0:1])
@@ -477,7 +485,7 @@
             pltpu.VMEM((views, ROWS, DIM), F32),
             pltpu.VMEM((PROTOS, DIM), F32),
         ),
-        in_specs=[vmem, vmem, vmem, vmem, hbm],
+        in_specs=[vmem, hbm, hbm, hbm, hbm],
         out_specs=(vmem, vmem, vmem, vmem),
         scratch_shapes=[
             pltpu.VMEM((views, NROW, DIM), BF16),
@@ -498,7 +506,7 @@
             pltpu.VMEM((128, 128), F32),
             pltpu.VMEM((views + 2, ROWS, 128), F32),
             pltpu.VMEM((views * ROWS, 128), F32),
-            dma(()),
+            dma(()), dma((6,)),
             dma((7, 5)), dma((7, 5)),
             dma((ITERS, DEVS)), dma((ITERS, DEVS)),
             dma((DEVS,)), dma((DEVS,)),
@@ -523,7 +531,7 @@
         ),
         in_specs=[vmem] * 4,
         out_specs=(hbm, hbm, pl.BlockSpec(memory_space=pltpu.SMEM), hbm, hbm, hbm, hbm),
-        scratch_shapes=[dma((6,))],
+        scratch_shapes=[dma((19,))],
         compiler_params=pltpu.CompilerParams(vmem_limit_bytes=1024 * 1024),
         name="write_out",
     )(*staged)

time: 72.2 us -> 71 us (0.983)
  Pallas kernels: 71.4 us -> 70.3 us
    pallas_call x1, Pallas kernels: 66 us -> 64.8 us  [local_step(): pl.pallas_call(body, out_shape=(pltpu.VMEM((2, ROWS, PROTOS), F32), pltpu...]
where the time goes in v6:
time: 71 us; the launch traced here: 70.9 us
  Pallas kernels  70.3 us (99%)
    pallas_call x1, Pallas kernels, local_step(): pl.pallas_call(body, out_shape=(pltpu.VMEM((2, ROWS, PROTOS), F32), pltpu...  64.8 us
    pallas_call x1, Pallas kernels, local_step(): pl.pallas_call(write_out, out_shape=(jax.ShapeDtypeStruct((ROWS, PROTOS),...  5.43 us

profile of v6, /device:TPU:0, one launch (start us, length us, event | category | flops | bytes accessed | tf_op | source)
XLA Modules:
  0.0 70.9 jit_solution(18021419811390610472)
XLA Ops:
  0.6 64.8 %swav_step.1 = (f32[2,64,8192]{2,1,0:T(8,128)S(1)}, f32[1,128]{1,0:T(1,128)S(1)}, f32[12,64,256]{2,1,0:T(8,128)S(1)}, f32[8192,256]{1,0:T(8,128)S(1)}) custom-call(s32[1,64]{1,0:T(1,128)} %bitcast.2, bf16[64,256]{1,0:T(8,128)(2,1)} %z1_hbm.1, bf16[64,256]{1,0:T(8,128)(2,1)} %z2_hbm.1, bf16[10,64,256]{2,1,0:T(8,128)(2,1)} %zs_hbm.1, bf16[8192,256]{1,0:T(8,128)(2,1)} %c_hbm.1), custom_call_target="tpu_custom_call" | custom-call | tf_op jit(solution)/shard_map/swav_step/pallas_call | solution.py:480
  65.5 5.4 %write_out.1 = (f32[64,8192]{1,0:T(8,128)}, f32[64,8192]{1,0:T(8,128)}, f32[1,1]{1,0:T(1,128)}, f32[64,256]{1,0:T(8,128)}, f32[64,256]{1,0:T(8,128)}, /*index=5*/f32[10,64,256]{2,1,0:T(8,128)}, f32[8192,256]{1,0:T(8,128)}) custom-call(f32[2,64,8192]{2,1,0:T(8,128)S(1)} %get-tuple-element.18.q_ref, f32[1,128]{1,0:T(1,128)S(1)} %get-tuple-element.19.loss_in, ...), custom_call_target="tpu_custom_call" | custom-call | tf_op jit(solution)/shard_map/write_out/pallas_call | solution.py:521

commit v7 on v6

--- a/solution.py
+++ b/solution.py
@@ -25,7 +25,6 @@
 F32 = jnp.float32
 BF16 = jnp.bfloat16
 UNITS = ((0, 1), (1, 1), (2, 4), (6, 4), (10, 2))
-SENT = 3
 EC = 512
 
 
@@ -273,12 +272,11 @@
     exp_views(10, 12)
     sink_close(2)
 
-    def acopy(src_dev, ch, half, to, kind):
-        lo = src_dev * OWN + ch * KC
-        if half is None:
-            rows = pl.ds(pl.multiple_of(lo, KC), KC)
-        else:
-            rows = pl.ds(pl.multiple_of(lo + half * (KC // 2), KC // 2), KC // 2)
+    def rows_of(dev, ch):
+        return pl.ds(pl.multiple_of(dev * OWN + ch * KC, KC), KC)
+
+    def acopy(dev, ch, to, kind):
+        rows = rows_of(dev, ch)
         return pltpu.make_async_remote_copy(
             src_ref=dcv.at[rows], dst_ref=dcv.at[rows], send_sem=asend.at[kind, ch],
             recv_sem=arecv.at[kind, ch], device_id=(to,), device_id_type=MESH)
@@ -296,29 +294,20 @@
             part = jnp.dot(g, zall[view], preferred_element_type=F32)
             acc = part if acc is None else acc + part
         dcv[pl.ds(pl.multiple_of(own0 + ch * KC, KC), KC)] = acc
-        acopy(me, ch, None, partner, 2).start()
+        acopy(me, ch, xn, 0).start()
+        acopy(me, ch, yn, 1).start()
+        acopy(me, ch, partner, 2).start()
         return carry
-
-    def dc_sent(ch, carry):
-        dc_chunk(ch, carry)
-        acopy(me, ch, None, xn, 0).start()
-        acopy(me, ch, None, yn, 1).start()
-        return carry
-    lax.fori_loop(0, SENT, dc_sent, 0)
-    lax.fori_loop(SENT, NCH, dc_chunk, 0)
-
-    def dc_again(i, carry):
-        which = i % 3
-        ch = SENT + i // 3
-        dev = me + (1 - which % 2) * (2 - 4 * xpos) + ((which + 1) // 2) * (4 - 8 * ypos)
-        lo = pl.multiple_of(dev * OWN + ch * KC, KC)
-        cc = cv[pl.ds(lo, KC)]
+    lax.fori_loop(0, NCH, dc_chunk, 0)
+
+    def dc_far(ch, carry):
+        cc = cv[rows_of(dg, ch)]
 
         def expo(view):
             return jnp.exp(nt_dot(cc, zall[view]) * (1.0 / TAU))
         gq, es = [], []
         for view in range(2):
-            vrow = vx[dev, view, :, pl.ds(pl.multiple_of(ch * KC, KC), KC)]
+            vrow = vx[dg, view, :, pl.ds(pl.multiple_of(ch * KC, KC), KC)]
             v = jnp.concatenate([jnp.broadcast_to(vrow[:, j * 128:(j + 1) * 128], (128, 128)).T
                                  for j in range(KC // 128)], axis=0)
             v = jnp.concatenate([v] * (NROW // 128), axis=1)
@@ -332,23 +321,19 @@
             g = (acf[view] * e - sub[view]).astype(BF16)
             part = jnp.dot(g, zall[view], preferred_element_type=F32)
             acc = part if acc is None else acc + part
-        dcv[pl.ds(lo, KC)] = acc
-        acopy(dev, ch, None, partner, 5 + which).start()
+        dcv[rows_of(dg, ch)] = acc
+        acopy(dg, ch, partner, 5).start()
         return carry
 
-    def relay(ch):
-        acopy(xn, ch, None, xn, 0).wait_recv()
-        acopy(xn, ch, 0, yn, 3).start()
-        acopy(xn, ch, None, partner, 5).start()
-        acopy(yn, ch, None, yn, 1).wait_recv()
-        acopy(yn, ch, 1, xn, 4).start()
-        acopy(yn, ch, None, partner, 6).start()
+    def forward(ch):
+        for dev, kind in ((xn, 0), (yn, 1)):
+            acopy(dev, ch, dev, kind).wait_recv()
+            acopy(dev, ch, partner, 3 + kind).start()
 
     bcast(*v_args, wait=True)
-    lax.fori_loop(0, 2, dc_again, 0)
-    relay(0)
-    lax.fori_loop(2, 3, dc_again, 0)
-    relay(1)
+    lax.fori_loop(0, NCH, dc_far, 0)
+    forward(0)
+    forward(1)
 
     lanes = pl.ds(pl.multiple_of((me // 2) * 128, 128), 128)
     for view in range(VIEWS):
@@ -391,17 +376,10 @@
         dz = jnp.dot(jnp.concatenate(parts, axis=0), cc, preferred_element_type=F32)
         dz_out[...] += dz.reshape(VIEWS, ROWS, DIM)
         return acc + fold(dot)
-    def far(ch):
-        acopy(dg, ch, 0, yn, 3).wait_recv()
-        acopy(dg, ch, 0, partner, 7).start()
-        acopy(dg, ch, 1, xn, 4).wait_recv()
-        acopy(dg, ch, 1, partner, 8).start()
-
     acc = lax.fori_loop(0, 6, row_chunk, jnp.zeros((8, PC), F32))
-    relay(2)
+    forward(2)
     acc = lax.fori_loop(6, 12, row_chunk, acc)
-    far(0)
-    far(1)
+    forward(3)
     acc = lax.fori_loop(12, PROTOS // PC, row_chunk, acc)
     cross = jnp.sum(jnp.sum(acc, axis=0, keepdims=True), axis=1, keepdims=True)
     px[me] = jnp.broadcast_to(cross, (1, 128))
@@ -413,31 +391,12 @@
         tot = tot + px[d]
     loss = -(tot[:, 0:1] * (1.0 / TAU) - log_sum) / (live_total * (2 + 2 * (VIEWS - 2)))
     loss_ref[...] = jnp.broadcast_to(loss, (1, 128))
-    far(2)
-
-    def drain_sent(ch, carry):
-        acopy(other(dg), ch, 0, partner, 7).wait_recv()
-        acopy(other(dg), ch, 1, partner, 8).wait_recv()
-        for kind in (0, 1):
-            acopy(me, ch, None, partner, kind).wait_send()
-        acopy(xn, ch, 0, yn, 3).wait_send()
-        acopy(yn, ch, 1, xn, 4).wait_send()
-        acopy(dg, ch, 0, partner, 7).wait_send()
-        acopy(dg, ch, 1, partner, 8).wait_send()
-        return carry
-
-    def drain_again(ch, carry):
-        acopy(other(dg), ch, None, partner, 7).wait_recv()
-        acopy(dg, ch, None, partner, 7).wait_send()
-        return carry
 
     def drain(ch, carry):
-        acopy(partner, ch, None, partner, 2).wait_recv()
-        acopy(other(xn), ch, None, partner, 5).wait_recv()
-        acopy(other(yn), ch, None, partner, 6).wait_recv()
-        acopy(me, ch, None, partner, 2).wait_send()
-        acopy(xn, ch, None, partner, 5).wait_send()
-        acopy(yn, ch, None, partner, 6).wait_send()
+        for kind, dev in ((2, me), (3, xn), (4, yn), (5, dg)):
+            acopy(other(dev), ch, partner, kind).wait_recv()
+        for kind, dev in ((0, me), (1, me), (2, me), (3, xn), (4, yn), (5, dg)):
+            acopy(dev, ch, partner, kind).wait_send()
         return carry
     for unit in range(len(UNITS)):
         for kind in range(7):
@@ -449,8 +408,6 @@
         bcast_drain(*r_args(it))
     bcast_drain(*l_args)
     lax.fori_loop(0, NCH, drain, 0)
-    lax.fori_loop(SENT, NCH, drain_again, 0)
-    lax.fori_loop(0, SENT, drain_sent, 0)
 
 
 def write_out(q_ref, loss_in, dz_ref, dc_ref, q1_hbm, q2_hbm, loss_ref, dz1_hbm, dz2_hbm, dzs_hbm, dc_hbm, sem):
@@ -512,7 +469,7 @@
             dma((DEVS,)), dma((DEVS,)),
             dma((DEVS,)), dma((DEVS,)),
             dma((2, DEVS)), dma((2, DEVS)),
-            dma((9, NCH)), dma((9, NCH)),
+            dma((6, NCH)), dma((6, NCH)),
         ],
         compiler_params=pltpu.CompilerParams(
             collective_id=0, has_side_effects=True, vmem_limit_bytes=48 * 1024 * 1024),

time: 71 us -> 69.4 us (0.977)
  Pallas kernels: 70.3 us -> 68.7 us
    pallas_call x1, Pallas kernels: 64.8 us -> 63.2 us  [local_step(): pl.pallas_call(body, out_shape=(pltpu.VMEM((2, ROWS, PROTOS), F32), pltpu...]
where the time goes in v7:
time: 69.4 us; the launch traced here: 69.3 us
  Pallas kernels  68.7 us (99%)
    pallas_call x1, Pallas kernels, local_step(): pl.pallas_call(body, out_shape=(pltpu.VMEM((2, ROWS, PROTOS), F32), pltpu...  63.2 us
    pallas_call x1, Pallas kernels, local_step(): pl.pallas_call(write_out, out_shape=(jax.ShapeDtypeStruct((ROWS, PROTOS),...  5.43 us

profile of v7, /device:TPU:0, one launch (start us, length us, event | category | flops | bytes accessed | tf_op | source)
XLA Modules:
  0.0 69.3 jit_solution(8649500108217167191)
XLA Ops:
  0.6 63.2 %swav_step.1 = (f32[2,64,8192]{2,1,0:T(8,128)S(1)}, f32[1,128]{1,0:T(1,128)S(1)}, f32[12,64,256]{2,1,0:T(8,128)S(1)}, f32[8192,256]{1,0:T(8,128)S(1)}) custom-call(s32[1,64]{1,0:T(1,128)} %bitcast.2, bf16[64,256]{1,0:T(8,128)(2,1)} %z1_hbm.1, bf16[64,256]{1,0:T(8,128)(2,1)} %z2_hbm.1, bf16[10,64,256]{2,1,0:T(8,128)(2,1)} %zs_hbm.1, bf16[8192,256]{1,0:T(8,128)(2,1)} %c_hbm.1), custom_call_target="tpu_custom_call" | custom-call | tf_op jit(solution)/shard_map/swav_step/pallas_call | solution.py:437
  63.9 5.4 %write_out.1 = (f32[64,8192]{1,0:T(8,128)}, f32[64,8192]{1,0:T(8,128)}, f32[1,1]{1,0:T(1,128)}, f32[64,256]{1,0:T(8,128)}, f32[64,256]{1,0:T(8,128)}, /*index=5*/f32[10,64,256]{2,1,0:T(8,128)}, f32[8192,256]{1,0:T(8,128)}) custom-call(f32[2,64,8192]{2,1,0:T(8,128)S(1)} %get-tuple-element.18.q_ref, f32[1,128]{1,0:T(1,128)S(1)} %get-tuple-element.19.loss_in, ...), custom_call_target="tpu_custom_call" | custom-call | tf_op jit(solution)/shard_map/write_out/pallas_call | solution.py:478

commit v8 on v7

--- a/solution.py
+++ b/solution.py
@@ -25,6 +25,7 @@
 F32 = jnp.float32
 BF16 = jnp.bfloat16
 UNITS = ((0, 1), (1, 1), (2, 4), (6, 4), (10, 2))
+FC = 512
 EC = 512
 
 
@@ -53,13 +54,33 @@
     my_rows = pl.ds(pl.multiple_of(me * ROWS, ROWS), ROWS)
     small = pl.ds(2, VIEWS - 2)
     own_copies = []
-    for src, dst in ((z1_hbm, zown.at[0]), (z2_hbm, zown.at[1]), (zs_hbm, zown.at[small]),
-                     (z1_hbm, zall.at[0, my_rows]), (z2_hbm, zall.at[1, my_rows]), (zs_hbm, zall.at[small, my_rows])):
-        own_copies.append(pltpu.make_async_copy(src, dst, isem.at[len(own_copies)]))
-        own_copies[-1].start()
+    for h in range(2):
+        half = pl.ds(h * 128, 128)
+        for src, dst in ((z1_hbm.at[:, half], zown.at[h, 0]),
+                         (z2_hbm.at[:, half], zown.at[h, 1]),
+                         (zs_hbm.at[:, :, half], zown.at[h, small]),
+                         (z1_hbm.at[:, half], zall.at[h, 0, my_rows]),
+                         (z2_hbm.at[:, half], zall.at[h, 1, my_rows]),
+                         (zs_hbm.at[:, :, half], zall.at[h, small, my_rows])):
+            own_copies.append(pltpu.make_async_copy(src, dst, isem.at[len(own_copies)]))
+            own_copies[-1].start()
     own0 = pl.multiple_of(me * OWN, OWN)
-    c_copy = pltpu.make_async_copy(c_hbm, cv, csem)
-    c_copy.start()
+    c_copies = []
+    for h in range(2):
+        c_copies.append(pltpu.make_async_copy(c_hbm.at[:, pl.ds(h * 128, 128)], cv.at[h], csem.at[h]))
+        c_copies[-1].start()
+
+    def halves(x0, x1):
+        return jnp.concatenate([x0, x1], axis=1)
+
+    def protos_at(rows):
+        return halves(cv[0, rows], cv[1, rows])
+
+    def view_rows(view):
+        return halves(zall[0, view], zall[1, view])
+
+    def own_rows():
+        return halves(zown[0].reshape(VIEWS * ROWS, 128), zown[1].reshape(VIEWS * ROWS, 128))
 
     barrier = pltpu.get_barrier_semaphore()
     for off in range(1, DEVS):
@@ -76,12 +97,12 @@
         lo, cnt = UNITS[unit]
         rows = pl.ds(pl.multiple_of(dev * ROWS, ROWS), ROWS)
         if cnt == 1:
-            return zall.at[lo, rows]
-        return zall.at[pl.ds(lo, cnt), rows]
+            return zall.at[:, lo, rows]
+        return zall.at[:, pl.ds(lo, cnt), rows]
 
     def zsrc(unit):
         lo, cnt = UNITS[unit]
-        return zown.at[lo] if cnt == 1 else zown.at[pl.ds(lo, cnt)]
+        return zown.at[:, lo] if cnt == 1 else zown.at[:, pl.ds(lo, cnt)]
 
     peers = (partner, xn, yn, dg)
 
@@ -163,11 +184,12 @@
         return out
 
     lacc[...] = jnp.zeros_like(lacc)
-    c_copy.wait()
+    for copy in c_copies:
+        copy.wait()
 
     def sum_chunk(ch, carry):
-        cc = cv[pl.ds(pl.multiple_of(ch * PC, PC), PC)]
-        scores = nt_dot(zown[...].reshape(VIEWS * ROWS, DIM), cc)
+        cc = protos_at(pl.ds(pl.multiple_of(ch * PC, PC), PC))
+        scores = nt_dot(own_rows(), cc)
         lacc[...] += lane_fold(jnp.exp(scores * (1.0 / TAU)))
         return carry
     def row_sums_out():
@@ -178,7 +200,7 @@
 
     def exp_block(view, ch):
         rows = pl.ds(pl.multiple_of(ch * EC, EC), EC)
-        scores = nt_dot(cv[pl.ds(pl.multiple_of(own0 + ch * EC, EC), EC)], zall[view])
+        scores = nt_dot(protos_at(pl.ds(pl.multiple_of(own0 + ch * EC, EC), EC)), view_rows(view))
         e = jnp.exp(scores * (1.0 / TAU))
         et[view, rows] = e
         return rows, e
@@ -291,7 +313,7 @@
         acc = None
         for view in range(VIEWS):
             g = (acf[view] * et[view, rows] - sub[view]).astype(BF16)
-            part = jnp.dot(g, zall[view], preferred_element_type=F32)
+            part = jnp.dot(g, view_rows(view), preferred_element_type=F32)
             acc = part if acc is None else acc + part
         dcv[pl.ds(pl.multiple_of(own0 + ch * KC, KC), KC)] = acc
         acopy(me, ch, xn, 0).start()
@@ -301,15 +323,16 @@
     lax.fori_loop(0, NCH, dc_chunk, 0)
 
     def dc_far(ch, carry):
-        cc = cv[rows_of(dg, ch)]
+        rows = pl.ds(pl.multiple_of(dg * OWN + ch * FC, FC), FC)
+        cc = protos_at(rows)
 
         def expo(view):
-            return jnp.exp(nt_dot(cc, zall[view]) * (1.0 / TAU))
+            return jnp.exp(nt_dot(cc, view_rows(view)) * (1.0 / TAU))
         gq, es = [], []
         for view in range(2):
-            vrow = vx[dg, view, :, pl.ds(pl.multiple_of(ch * KC, KC), KC)]
+            vrow = vx[dg, view, :, pl.ds(pl.multiple_of(ch * FC, FC), FC)]
             v = jnp.concatenate([jnp.broadcast_to(vrow[:, j * 128:(j + 1) * 128], (128, 128)).T
-                                 for j in range(KC // 128)], axis=0)
+                                 for j in range(FC // 128)], axis=0)
             v = jnp.concatenate([v] * (NROW // 128), axis=1)
             e = expo(view)
             es.append(e)
@@ -319,10 +342,11 @@
         for view in range(VIEWS):
             e = es[view] if view < 2 else expo(view)
             g = (acf[view] * e - sub[view]).astype(BF16)
-            part = jnp.dot(g, zall[view], preferred_element_type=F32)
+            part = jnp.dot(g, view_rows(view), preferred_element_type=F32)
             acc = part if acc is None else acc + part
-        dcv[rows_of(dg, ch)] = acc
-        acopy(dg, ch, partner, 5).start()
+        dcv[rows] = acc
+        for part in range(FC // KC):
+            acopy(dg, ch * (FC // KC) + part, partner, 5).start()
         return carry
 
     def forward(ch):
@@ -331,7 +355,7 @@
             acopy(dev, ch, partner, 3 + kind).start()
 
     bcast(*v_args, wait=True)
-    lax.fori_loop(0, NCH, dc_far, 0)
+    lax.fori_loop(0, OWN // FC, dc_far, 0)
     forward(0)
     forward(1)
 
@@ -352,8 +376,8 @@
 
     def row_chunk(ch, acc):
         cols = pl.ds(pl.multiple_of(ch * PC, PC), PC)
-        cc = cv[pl.ds(pl.multiple_of(ch * PC, PC), PC)]
-        scores = nt_dot(zown[...].reshape(VIEWS * ROWS, DIM), cc)
+        cc = protos_at(pl.ds(pl.multiple_of(ch * PC, PC), PC))
+        scores = nt_dot(own_rows(), cc)
         dev = ch // (OWN // PC)
         half = pl.ds(pl.multiple_of((ch % (OWN // PC)) * PC, PC), PC)
         e_large, q_large = [], []
@@ -445,9 +469,9 @@
         in_specs=[vmem, hbm, hbm, hbm, hbm],
         out_specs=(vmem, vmem, vmem, vmem),
         scratch_shapes=[
-            pltpu.VMEM((views, NROW, DIM), BF16),
-            pltpu.VMEM((views, ROWS, DIM), BF16),
-            pltpu.VMEM((PROTOS, DIM), BF16),
+            pltpu.VMEM((2, views, NROW, 128), BF16),
+            pltpu.VMEM((2, views, ROWS, 128), BF16),
+            pltpu.VMEM((2, PROTOS, 128), BF16),
             pltpu.VMEM((views, OWN, NROW), F32),
             pltpu.VMEM((2, OWN, NROW), F32),
             pltpu.VMEM((2, OWN, 128), F32),
@@ -463,7 +487,7 @@
             pltpu.VMEM((128, 128), F32),
             pltpu.VMEM((views + 2, ROWS, 128), F32),
             pltpu.VMEM((views * ROWS, 128), F32),
-            dma(()), dma((6,)),
+            dma((2,)), dma((12,)),
             dma((7, 5)), dma((7, 5)),
             dma((ITERS, DEVS)), dma((ITERS, DEVS)),
             dma((DEVS,)), dma((DEVS,)),

time: 69.4 us -> 69.5 us (level)
  no operation moved by 1% of the time
where the time goes in v8:
time: 69.5 us; the launch traced here: 69.4 us
  Pallas kernels  68.8 us (99%)
    pallas_call x1, Pallas kernels, local_step(): pl.pallas_call(body, out_shape=(pltpu.VMEM((2, ROWS, PROTOS), F32), pltpu...  63.3 us
    pallas_call x1, Pallas kernels, local_step(): pl.pallas_call(write_out, out_shape=(jax.ShapeDtypeStruct((ROWS, PROTOS),...  5.43 us

profile of v8, /device:TPU:0, one launch (start us, length us, event | category | flops | bytes accessed | tf_op | source)
XLA Modules:
  0.0 69.4 jit_solution(280988007182920701)
XLA Ops:
  0.6 63.3 %swav_step.1 = (f32[2,64,8192]{2,1,0:T(8,128)S(1)}, f32[1,128]{1,0:T(1,128)S(1)}, f32[12,64,256]{2,1,0:T(8,128)S(1)}, f32[8192,256]{1,0:T(8,128)S(1)}) custom-call(s32[1,64]{1,0:T(1,128)} %bitcast.2, bf16[64,256]{1,0:T(8,128)(2,1)} %z1_hbm.1, bf16[64,256]{1,0:T(8,128)(2,1)} %z2_hbm.1, bf16[10,64,256]{2,1,0:T(8,128)(2,1)} %zs_hbm.1, bf16[8192,256]{1,0:T(8,128)(2,1)} %c_hbm.1), custom_call_target="tpu_custom_call" | custom-call | tf_op jit(solution)/shard_map/swav_step/pallas_call | solution.py:461
  64.0 5.4 %write_out.1 = (f32[64,8192]{1,0:T(8,128)}, f32[64,8192]{1,0:T(8,128)}, f32[1,1]{1,0:T(1,128)}, f32[64,256]{1,0:T(8,128)}, f32[64,256]{1,0:T(8,128)}, /*index=5*/f32[10,64,256]{2,1,0:T(8,128)}, f32[8192,256]{1,0:T(8,128)}) custom-call(f32[2,64,8192]{2,1,0:T(8,128)S(1)} %get-tuple-element.18.q_ref, f32[1,128]{1,0:T(1,128)S(1)} %get-tuple-element.19.loss_in, ...), custom_call_target="tpu_custom_call" | custom-call | tf_op jit(solution)/shard_map/write_out/pallas_call | solution.py:502

commit v9 on v8

--- a/solution.py
+++ b/solution.py
@@ -20,11 +20,12 @@
 OWN = PROTOS // DEVS
 KC = 256
 NCH = OWN // KC
+KEPT = 8
 PC = 512
 MESH = pl.DeviceIdType.MESH
 F32 = jnp.float32
 BF16 = jnp.bfloat16
-UNITS = ((0, 1), (1, 1), (2, 4), (6, 4), (10, 2))
+UNITS = ((0, 1), (1, 1), (2, 5), (7, 3), (10, 2))
 FC = 512
 EC = 512
 
@@ -35,7 +36,7 @@
 
 def body(mask_ref, z1_hbm, z2_hbm, zs_hbm, c_hbm,
          q_out, loss_ref, dz_out, dcv,
-         zall, zown, cv, et, a0, vb, vx, rx, lx, mx, px,
+         zall, zown, cv, et, sst, vb, vx, rx, lx, mx, px,
          mvec, wvec, acf, cf, ct, ab, lacc,
          csem, isem, zsend, zrecv, rsend, rrecv, lsend, lrecv, vsend, vrecv, psend, precv,
          asend, arecv):
@@ -187,10 +188,12 @@
     for copy in c_copies:
         copy.wait()
 
-    def sum_chunk(ch, carry):
+    def sum_chunk(ch, carry, keep=False):
         cc = protos_at(pl.ds(pl.multiple_of(ch * PC, PC), PC))
         scores = nt_dot(own_rows(), cc)
         lacc[...] += lane_fold(jnp.exp(scores * (1.0 / TAU)))
+        if keep:
+            sst[ch - (PROTOS // PC - KEPT)] = scores
         return carry
     def row_sums_out():
         for view in range(VIEWS):
@@ -223,11 +226,7 @@
 
     SB = 128
 
-    def sq_step(i, carry):
-        rows, e = exp_block(i // 2, i % 2)
-        a0[i // 2, rows] = e * e
-        return carry
-    lax.fori_loop(0, 2 * (OWN // EC), sq_step, 0)
+    exp_views(0, 2)
 
     def sink_pass(it):
         scale = (1.0 if it == 0 else live_total) * (1.0 / PROTOS)
@@ -236,7 +235,8 @@
             rows = pl.ds(pl.multiple_of(blk * SB, SB), SB)
             out = []
             for view in range(2):
-                a = a0[view, rows]
+                e = et[view, rows]
+                a = e * e
                 w = mvec[...] if it == 0 else wvec[view]
                 colsum = jnp.sum(a * w, axis=1, keepdims=True)
                 v = scale / colsum
@@ -260,14 +260,14 @@
 
     sink_pass(0)
     zstart(3)
-    lax.fori_loop(8, PROTOS // PC, sum_chunk, 0)
-    row_sums_out()
+    lax.fori_loop(PROTOS // PC - KEPT, PROTOS // PC, functools.partial(sum_chunk, keep=True), 0)
     zforward((2,))
     sink_close(0)
     sink_pass(1)
+    row_sums_out()
     zstart(4)
     zfinish((2,))
-    exp_views(2, 6)
+    exp_views(2, 7)
     zforward((3,))
     sink_close(1)
     sink_pass(2)
@@ -288,7 +288,7 @@
             vx[me, view, :, blk * 128:(blk + 1) * 128] = vt[0:1, :]
     bcast(*v_args, wait=False)
     zfinish((3,))
-    exp_views(6, 10)
+    exp_views(7, 10)
     zforward((4,))
     zfinish((4,))
     exp_views(10, 12)
@@ -308,7 +308,8 @@
         gq = []
         for view in range(2):
             v = jnp.concatenate([vb[view, rows]] * (NROW // 128), axis=1)
-            gq.append((wvec[view] * grad_scale) * (v * a0[view, rows]))
+            e = et[view, rows]
+            gq.append((wvec[view] * grad_scale) * (v * (e * e)))
         sub = [gq[1], gq[0]] + [gq[0] + gq[1]] * (VIEWS - 2)
         acc = None
         for view in range(VIEWS):
@@ -374,15 +375,22 @@
     def wide(x):
         return jnp.concatenate([x] * (PC // 128), axis=1)
 
-    def row_chunk(ch, acc):
+    def row_chunk(ch, acc, kept=False):
         cols = pl.ds(pl.multiple_of(ch * PC, PC), PC)
         cc = protos_at(pl.ds(pl.multiple_of(ch * PC, PC), PC))
-        scores = nt_dot(own_rows(), cc)
+        if kept:
+            def score(view):
+                return sst[ch - (PROTOS // PC - KEPT), view * ROWS:(view + 1) * ROWS]
+        else:
+            scores = nt_dot(own_rows(), cc)
+
+            def score(view):
+                return scores[view * ROWS:(view + 1) * ROWS]
         dev = ch // (OWN // PC)
         half = pl.ds(pl.multiple_of((ch % (OWN // PC)) * PC, PC), PC)
         e_large, q_large = [], []
         for view in range(2):
-            e = jnp.exp(scores[view * ROWS:(view + 1) * ROWS] * (1.0 / TAU))
+            e = jnp.exp(score(view) * (1.0 / TAU))
             q = wide(ab[VIEWS + view]) * (vx[dev, view, :, half] * (e * e))
             q_out[view, :, cols] = q
             e_large.append(e)
@@ -393,18 +401,19 @@
                  (wide(ab[1]) * e_large[1] - q_large[0] * grad_scale).astype(BF16)]
         s_sum = None
         for view in range(2, VIEWS):
-            s = scores[view * ROWS:(view + 1) * ROWS]
+            s = score(view)
             s_sum = s if s_sum is None else s_sum + s
             parts.append((wide(ab[view]) * jnp.exp(s * (1.0 / TAU)) - gq_sum).astype(BF16))
-        dot = q_large[1] * scores[0:ROWS] + q_large[0] * scores[ROWS:2 * ROWS] + q_sum * s_sum
+        dot = q_large[1] * score(0) + q_large[0] * score(1) + q_sum * s_sum
         dz = jnp.dot(jnp.concatenate(parts, axis=0), cc, preferred_element_type=F32)
         dz_out[...] += dz.reshape(VIEWS, ROWS, DIM)
         return acc + fold(dot)
-    acc = lax.fori_loop(0, 6, row_chunk, jnp.zeros((8, PC), F32))
+    acc = lax.fori_loop(0, PROTOS // PC - KEPT, row_chunk, jnp.zeros((8, PC), F32))
     forward(2)
-    acc = lax.fori_loop(6, 12, row_chunk, acc)
+    row_kept = functools.partial(row_chunk, kept=True)
+    acc = lax.fori_loop(PROTOS // PC - KEPT, PROTOS // PC - 2, row_kept, acc)
     forward(3)
-    acc = lax.fori_loop(12, PROTOS // PC, row_chunk, acc)
+    acc = lax.fori_loop(PROTOS // PC - 2, PROTOS // PC, row_kept, acc)
     cross = jnp.sum(jnp.sum(acc, axis=0, keepdims=True), axis=1, keepdims=True)
     px[me] = jnp.broadcast_to(cross, (1, 128))
     bcast(*p_args, wait=False)
@@ -473,7 +482,7 @@
             pltpu.VMEM((2, views, ROWS, 128), BF16),
             pltpu.VMEM((2, PROTOS, 128), BF16),
             pltpu.VMEM((views, OWN, NROW), F32),
-            pltpu.VMEM((2, OWN, NROW), F32),
+            pltpu.VMEM((KEPT, views * ROWS, PC), F32),
             pltpu.VMEM((2, OWN, 128), F32),
             pltpu.VMEM((DEVS, 2, 1, OWN), F32),
             pltpu.VMEM((ITERS, DEVS, 1, 2 * NROW), F32),
@@ -496,7 +505,7 @@
             dma((6, NCH)), dma((6, NCH)),
         ],
         compiler_params=pltpu.CompilerParams(
-            collective_id=0, has_side_effects=True, vmem_limit_bytes=48 * 1024 * 1024),
+            collective_id=0, has_side_effects=True, vmem_limit_bytes=50 * 1024 * 1024),
         name="swav_step",
     )(live_mask.reshape(1, ROWS), z_one, z_two, z_small, protos)
     q_one, q_two, loss, dz_one, dz_two, dz_small, d_protos = pl.pallas_call(

time: 69.5 us -> 66.2 us (0.953)
  Pallas kernels: 68.8 us -> 65.5 us
    pallas_call x1, Pallas kernels: 63.3 us -> 60 us  [local_step(): pl.pallas_call(body, out_shape=(pltpu.VMEM((2, ROWS, PROTOS), F32), pltpu...]
where the time goes in v9:
time: 66.2 us; the launch traced here: 66.1 us
  Pallas kernels  65.5 us (99%)
    pallas_call x1, Pallas kernels, local_step(): pl.pallas_call(body, out_shape=(pltpu.VMEM((2, ROWS, PROTOS), F32), pltpu...  60 us
    pallas_call x1, Pallas kernels, local_step(): pl.pallas_call(write_out, out_shape=(jax.ShapeDtypeStruct((ROWS, PROTOS),...  5.43 us

profile of v9, /device:TPU:0, one launch (start us, length us, event | category | flops | bytes accessed | tf_op | source)
XLA Modules:
  0.0 66.1 jit_solution(13459939936265983642)
XLA Ops:
  0.6 60.0 %swav_step.1 = (f32[2,64,8192]{2,1,0:T(8,128)S(1)}, f32[1,128]{1,0:T(1,128)S(1)}, f32[12,64,256]{2,1,0:T(8,128)S(1)}, f32[8192,256]{1,0:T(8,128)S(1)}) custom-call(s32[1,64]{1,0:T(1,128)} %bitcast.2, bf16[64,256]{1,0:T(8,128)(2,1)} %z1_hbm.1, bf16[64,256]{1,0:T(8,128)(2,1)} %z2_hbm.1, bf16[10,64,256]{2,1,0:T(8,128)(2,1)} %zs_hbm.1, bf16[8192,256]{1,0:T(8,128)(2,1)} %c_hbm.1), custom_call_target="tpu_custom_call" | custom-call | tf_op jit(solution)/shard_map/swav_step/pallas_call | solution.py:470
  60.7 5.4 %write_out.1 = (f32[64,8192]{1,0:T(8,128)}, f32[64,8192]{1,0:T(8,128)}, f32[1,1]{1,0:T(1,128)}, f32[64,256]{1,0:T(8,128)}, f32[64,256]{1,0:T(8,128)}, /*index=5*/f32[10,64,256]{2,1,0:T(8,128)}, f32[8192,256]{1,0:T(8,128)}) custom-call(f32[2,64,8192]{2,1,0:T(8,128)S(1)} %get-tuple-element.18.q_ref, f32[1,128]{1,0:T(1,128)S(1)} %get-tuple-element.19.loss_in, ...), custom_call_target="tpu_custom_call" | custom-call | tf_op jit(solution)/shard_map/write_out/pallas_call | solution.py:511

commit v10 on v9

--- a/solution.py
+++ b/solution.py
@@ -26,7 +26,6 @@
 F32 = jnp.float32
 BF16 = jnp.bfloat16
 UNITS = ((0, 1), (1, 1), (2, 5), (7, 3), (10, 2))
-FC = 512
 EC = 512
 
 
@@ -34,11 +33,11 @@
     return lax.dot_general(a, b, (((1,), (1,)), ((), ())), preferred_element_type=F32)
 
 
-def body(mask_ref, z1_hbm, z2_hbm, zs_hbm, c_hbm,
+def body(mask_hbm, z1_hbm, z2_hbm, zs_hbm, c_hbm,
          q_out, loss_ref, dz_out, dcv,
          zall, zown, cv, et, sst, vb, vx, rx, lx, mx, px,
          mvec, wvec, acf, cf, ct, ab, lacc,
-         csem, isem, zsend, zrecv, rsend, rrecv, lsend, lrecv, vsend, vrecv, psend, precv,
+         mask_ref, csem, isem, zsend, zrecv, rsend, rrecv, lsend, lrecv, vsend, vrecv, psend, precv,
          asend, arecv):
     me = lax.axis_index("data")
     core = me % 2
@@ -66,6 +65,8 @@
             own_copies.append(pltpu.make_async_copy(src, dst, isem.at[len(own_copies)]))
             own_copies[-1].start()
     own0 = pl.multiple_of(me * OWN, OWN)
+    own_copies.append(pltpu.make_async_copy(mask_hbm, mask_ref, isem.at[12]))
+    own_copies[-1].start()
     c_copies = []
     for h in range(2):
         c_copies.append(pltpu.make_async_copy(c_hbm.at[:, pl.ds(h * 128, 128)], cv.at[h], csem.at[h]))
@@ -86,13 +87,6 @@
     barrier = pltpu.get_barrier_semaphore()
     for off in range(1, DEVS):
         pl.semaphore_signal(barrier, inc=1, device_id=((me + off) % DEVS,), device_id_type=MESH)
-
-    mrow = mask_ref[...].astype(F32)
-    sel = (lax.broadcasted_iota(jnp.int32, (ROWS, 128), 1)
-           == lax.broadcasted_iota(jnp.int32, (ROWS, 128), 0) + ROWS * core)
-    mplaced = jnp.dot(jnp.broadcast_to(mrow, (8, ROWS)).astype(BF16), sel.astype(BF16),
-                      preferred_element_type=F32)
-    mx[me] = mplaced[0:1, :]
 
     def zdst(unit, dev):
         lo, cnt = UNITS[unit]
@@ -169,6 +163,14 @@
 
     for copy in own_copies:
         copy.wait()
+
+    mrow = mask_ref[...].astype(F32)
+    sel = (lax.broadcasted_iota(jnp.int32, (ROWS, 128), 1)
+           == lax.broadcasted_iota(jnp.int32, (ROWS, 128), 0) + ROWS * core)
+    mplaced = jnp.dot(jnp.broadcast_to(mrow, (8, ROWS)).astype(BF16), sel.astype(BF16),
+                      preferred_element_type=F32)
+    mx[me] = mplaced[0:1, :]
+
     pl.semaphore_wait(barrier, DEVS - 1)
     zstart(0)
     zstart(1)
@@ -201,17 +203,17 @@
             lx[me, view] = jnp.sum(jnp.concatenate([la, la], axis=0).T, axis=0, keepdims=True)
         bcast(*l_args, wait=False)
 
-    def exp_block(view, ch):
+    def exp_block(view, ch, base):
         rows = pl.ds(pl.multiple_of(ch * EC, EC), EC)
-        scores = nt_dot(protos_at(pl.ds(pl.multiple_of(own0 + ch * EC, EC), EC)), view_rows(view))
+        scores = nt_dot(protos_at(pl.ds(pl.multiple_of(base + ch * EC, EC), EC)), view_rows(view))
         e = jnp.exp(scores * (1.0 / TAU))
         et[view, rows] = e
         return rows, e
 
-    def exp_views(lo, hi):
+    def exp_views(lo, hi, base=own0):
         def step(view, carry):
             for ch in range(OWN // EC):
-                exp_block(view, ch)
+                exp_block(view, ch, base)
             return carry
         lax.fori_loop(lo, hi, step, 0)
 
@@ -303,7 +305,7 @@
             src_ref=dcv.at[rows], dst_ref=dcv.at[rows], send_sem=asend.at[kind, ch],
             recv_sem=arecv.at[kind, ch], device_id=(to,), device_id_type=MESH)
 
-    def dc_chunk(ch, carry):
+    def dc_chunk(dev, ch):
         rows = pl.ds(pl.multiple_of(ch * KC, KC), KC)
         gq = []
         for view in range(2):
@@ -316,38 +318,19 @@
             g = (acf[view] * et[view, rows] - sub[view]).astype(BF16)
             part = jnp.dot(g, view_rows(view), preferred_element_type=F32)
             acc = part if acc is None else acc + part
-        dcv[pl.ds(pl.multiple_of(own0 + ch * KC, KC), KC)] = acc
+        dcv[rows_of(dev, ch)] = acc
+
+    def dc_own(ch, carry):
+        dc_chunk(me, ch)
         acopy(me, ch, xn, 0).start()
         acopy(me, ch, yn, 1).start()
         acopy(me, ch, partner, 2).start()
         return carry
-    lax.fori_loop(0, NCH, dc_chunk, 0)
+    lax.fori_loop(0, NCH, dc_own, 0)
 
     def dc_far(ch, carry):
-        rows = pl.ds(pl.multiple_of(dg * OWN + ch * FC, FC), FC)
-        cc = protos_at(rows)
-
-        def expo(view):
-            return jnp.exp(nt_dot(cc, view_rows(view)) * (1.0 / TAU))
-        gq, es = [], []
-        for view in range(2):
-            vrow = vx[dg, view, :, pl.ds(pl.multiple_of(ch * FC, FC), FC)]
-            v = jnp.concatenate([jnp.broadcast_to(vrow[:, j * 128:(j + 1) * 128], (128, 128)).T
-                                 for j in range(FC // 128)], axis=0)
-            v = jnp.concatenate([v] * (NROW // 128), axis=1)
-            e = expo(view)
-            es.append(e)
-            gq.append((wvec[view] * grad_scale) * (v * (e * e)))
-        sub = [gq[1], gq[0]] + [gq[0] + gq[1]] * (VIEWS - 2)
-        acc = None
-        for view in range(VIEWS):
-            e = es[view] if view < 2 else expo(view)
-            g = (acf[view] * e - sub[view]).astype(BF16)
-            part = jnp.dot(g, view_rows(view), preferred_element_type=F32)
-            acc = part if acc is None else acc + part
-        dcv[rows] = acc
-        for part in range(FC // KC):
-            acopy(dg, ch * (FC // KC) + part, partner, 5).start()
+        dc_chunk(dg, ch)
+        acopy(dg, ch, partner, 5).start()
         return carry
 
     def forward(ch):
@@ -356,7 +339,12 @@
             acopy(dev, ch, partner, 3 + kind).start()
 
     bcast(*v_args, wait=True)
-    lax.fori_loop(0, OWN // FC, dc_far, 0)
+    for view in range(2):
+        for blk in range(OWN // 128):
+            lanes = slice(blk * 128, (blk + 1) * 128)
+            vb[view, lanes] = jnp.broadcast_to(vx[dg, view, :, lanes], (128, 128)).T
+    exp_views(0, VIEWS, dg * OWN)
+    lax.fori_loop(0, NCH, dc_far, 0)
     forward(0)
     forward(1)
 
@@ -475,7 +463,7 @@
             pltpu.VMEM((views, ROWS, DIM), F32),
             pltpu.VMEM((PROTOS, DIM), F32),
         ),
-        in_specs=[vmem, hbm, hbm, hbm, hbm],
+        in_specs=[hbm] * 5,
         out_specs=(vmem, vmem, vmem, vmem),
         scratch_shapes=[
             pltpu.VMEM((2, views, NROW, 128), BF16),
@@ -496,7 +484,8 @@
             pltpu.VMEM((128, 128), F32),
             pltpu.VMEM((views + 2, ROWS, 128), F32),
             pltpu.VMEM((views * ROWS, 128), F32),
-            dma((2,)), dma((12,)),
+            pltpu.VMEM((1, ROWS), jnp.int32),
+            dma((2,)), dma((13,)),
             dma((7, 5)), dma((7, 5)),
             dma((ITERS, DEVS)), dma((ITERS, DEVS)),
             dma((DEVS,)), dma((DEVS,)),

time: 66.2 us -> 65.7 us (level)
  no operation moved by 1% of the time
where the time goes in v10:
time: 65.7 us; the launch traced here: 65.6 us
  Pallas kernels  65 us (99%)
    pallas_call x1, Pallas kernels, local_step(): pl.pallas_call(body, out_shape=(pltpu.VMEM((2, ROWS, PROTOS), F32), pltpu...  59.6 us
    pallas_call x1, Pallas kernels, local_step(): pl.pallas_call(write_out, out_shape=(jax.ShapeDtypeStruct((ROWS, PROTOS),...  5.43 us

profile of v10, /device:TPU:0, one launch (start us, length us, event | category | flops | bytes accessed | tf_op | source)
XLA Modules:
  0.0 65.6 jit_solution(10266191041673061443)
XLA Ops:
  0.6 59.6 %swav_step.1 = (f32[2,64,8192]{2,1,0:T(8,128)S(1)}, f32[1,128]{1,0:T(1,128)S(1)}, f32[12,64,256]{2,1,0:T(8,128)S(1)}, f32[8192,256]{1,0:T(8,128)S(1)}) custom-call(s32[1,64]{1,0:T(1,128)} %bitcast.2, bf16[64,256]{1,0:T(8,128)(2,1)} %z1_hbm.1, bf16[64,256]{1,0:T(8,128)(2,1)} %z2_hbm.1, bf16[10,64,256]{2,1,0:T(8,128)(2,1)} %zs_hbm.1, bf16[8192,256]{1,0:T(8,128)(2,1)} %c_hbm.1), custom_call_target="tpu_custom_call" | custom-call | tf_op jit(solution)/shard_map/swav_step/pallas_call | solution.py:458
  60.2 5.4 %write_out.1 = (f32[64,8192]{1,0:T(8,128)}, f32[64,8192]{1,0:T(8,128)}, f32[1,1]{1,0:T(1,128)}, f32[64,256]{1,0:T(8,128)}, f32[64,256]{1,0:T(8,128)}, /*index=5*/f32[10,64,256]{2,1,0:T(8,128)}, f32[8192,256]{1,0:T(8,128)}) custom-call(f32[2,64,8192]{2,1,0:T(8,128)S(1)} %get-tuple-element.18.q_ref, f32[1,128]{1,0:T(1,128)S(1)} %get-tuple-element.19.loss_in, ...), custom_call_target="tpu_custom_call" | custom-call | tf_op jit(solution)/shard_map/write_out/pallas_call | solution.py:500

commit v11 on v10

--- a/solution.py
+++ b/solution.py
@@ -36,7 +36,7 @@
 def body(mask_hbm, z1_hbm, z2_hbm, zs_hbm, c_hbm,
          q_out, loss_ref, dz_out, dcv,
          zall, zown, cv, et, sst, vb, vx, rx, lx, mx, px,
-         mvec, wvec, acf, cf, ct, ab, lacc,
+         mvec, wvec, acf, cf, ct, ab, lacc, gbuf,
          mask_ref, csem, isem, zsend, zrecv, rsend, rrecv, lsend, lrecv, vsend, vrecv, psend, precv,
          asend, arecv):
     me = lax.axis_index("data")
@@ -360,43 +360,41 @@
 
     dz_out[...] = jnp.zeros_like(dz_out)
 
-    def wide(x):
-        return jnp.concatenate([x] * (PC // 128), axis=1)
-
     def row_chunk(ch, acc, kept=False):
-        cols = pl.ds(pl.multiple_of(ch * PC, PC), PC)
         cc = protos_at(pl.ds(pl.multiple_of(ch * PC, PC), PC))
-        if kept:
-            def score(view):
-                return sst[ch - (PROTOS // PC - KEPT), view * ROWS:(view + 1) * ROWS]
-        else:
+        if not kept:
             scores = nt_dot(own_rows(), cc)
 
-            def score(view):
-                return scores[view * ROWS:(view + 1) * ROWS]
+        def score(view, sub):
+            rows, lanes = slice(view * ROWS, (view + 1) * ROWS), slice(sub * 128, (sub + 1) * 128)
+            return sst[ch - (PROTOS // PC - KEPT), rows, lanes] if kept else scores[rows, lanes]
         dev = ch // (OWN // PC)
-        half = pl.ds(pl.multiple_of((ch % (OWN // PC)) * PC, PC), PC)
-        e_large, q_large = [], []
-        for view in range(2):
-            e = jnp.exp(score(view) * (1.0 / TAU))
-            q = wide(ab[VIEWS + view]) * (vx[dev, view, :, half] * (e * e))
-            q_out[view, :, cols] = q
-            e_large.append(e)
-            q_large.append(q)
-        q_sum = q_large[0] + q_large[1]
-        gq_sum = q_sum * grad_scale
-        parts = [(wide(ab[0]) * e_large[0] - q_large[1] * grad_scale).astype(BF16),
-                 (wide(ab[1]) * e_large[1] - q_large[0] * grad_scale).astype(BF16)]
-        s_sum = None
-        for view in range(2, VIEWS):
-            s = score(view)
-            s_sum = s if s_sum is None else s_sum + s
-            parts.append((wide(ab[view]) * jnp.exp(s * (1.0 / TAU)) - gq_sum).astype(BF16))
-        dot = q_large[1] * score(0) + q_large[0] * score(1) + q_sum * s_sum
-        dz = jnp.dot(jnp.concatenate(parts, axis=0), cc, preferred_element_type=F32)
+        for sub in range(PC // 128):
+            lanes = pl.ds(pl.multiple_of((ch % (OWN // PC)) * PC + sub * 128, 128), 128)
+            cols = pl.ds(pl.multiple_of(ch * PC + sub * 128, 128), 128)
+            s0, s1 = score(0, sub), score(1, sub)
+            e0, e1 = jnp.exp(s0 * (1.0 / TAU)), jnp.exp(s1 * (1.0 / TAU))
+            q0 = ab[VIEWS] * (vx[dev, 0, :, lanes] * (e0 * e0))
+            q1 = ab[VIEWS + 1] * (vx[dev, 1, :, lanes] * (e1 * e1))
+            q_out[0, :, cols] = q0
+            q_out[1, :, cols] = q1
+            gbuf[sub, 0:ROWS] = (ab[0] * e0 - q1 * grad_scale).astype(BF16)
+            gbuf[sub, ROWS:2 * ROWS] = (ab[1] * e1 - q0 * grad_scale).astype(BF16)
+            cross = q1 * s0 + q0 * s1
+            q_sum = q0 + q1
+            gq_sum = q_sum * grad_scale
+            s_sum = None
+            for view in range(2, VIEWS):
+                s = score(view, sub)
+                s_sum = s if s_sum is None else s_sum + s
+                gbuf[sub, view * ROWS:(view + 1) * ROWS] = (
+                    ab[view] * jnp.exp(s * (1.0 / TAU)) - gq_sum).astype(BF16)
+            acc = acc + fold(cross + q_sum * s_sum)
+        g = jnp.concatenate([gbuf[sub] for sub in range(PC // 128)], axis=1)
+        dz = jnp.dot(g, cc, preferred_element_type=F32)
         dz_out[...] += dz.reshape(VIEWS, ROWS, DIM)
-        return acc + fold(dot)
-    acc = lax.fori_loop(0, PROTOS // PC - KEPT, row_chunk, jnp.zeros((8, PC), F32))
+        return acc
+    acc = lax.fori_loop(0, PROTOS // PC - KEPT, row_chunk, jnp.zeros((8, 128), F32))
     forward(2)
     row_kept = functools.partial(row_chunk, kept=True)
     acc = lax.fori_loop(PROTOS // PC - KEPT, PROTOS // PC - 2, row_kept, acc)
@@ -484,6 +482,7 @@
             pltpu.VMEM((128, 128), F32),
             pltpu.VMEM((views + 2, ROWS, 128), F32),
             pltpu.VMEM((views * ROWS, 128), F32),
+            pltpu.VMEM((PC // 128, views * ROWS, 128), BF16),
             pltpu.VMEM((1, ROWS), jnp.int32),
             dma((2,)), dma((13,)),
             dma((7, 5)), dma((7, 5)),

time: 65.7 us -> 66.8 us (1.017)
  Pallas kernels: 65 us -> 66.1 us
    pallas_call x1, Pallas kernels: 59.6 us -> 60.6 us  [local_step(): pl.pallas_call(body, out_shape=(pltpu.VMEM((2, ROWS, PROTOS), F32), pltpu...]
where the time goes in v11:
time: 66.8 us; the launch traced here: 66.7 us
  Pallas kernels  66.1 us (99%)
    pallas_call x1, Pallas kernels, local_step(): pl.pallas_call(body, out_shape=(pltpu.VMEM((2, ROWS, PROTOS), F32), pltpu...  60.6 us
    pallas_call x1, Pallas kernels, local_step(): pl.pallas_call(write_out, out_shape=(jax.ShapeDtypeStruct((ROWS, PROTOS),...  5.43 us

profile of v11, /device:TPU:0, one launch (start us, length us, event | category | flops | bytes accessed | tf_op | source)
XLA Modules:
  0.0 66.7 jit_solution(1633808151387483826)
XLA Ops:
  0.6 60.6 %swav_step.1 = (f32[2,64,8192]{2,1,0:T(8,128)S(1)}, f32[1,128]{1,0:T(1,128)S(1)}, f32[12,64,256]{2,1,0:T(8,128)S(1)}, f32[8192,256]{1,0:T(8,128)S(1)}) custom-call(s32[1,64]{1,0:T(1,128)} %bitcast.2, bf16[64,256]{1,0:T(8,128)(2,1)} %z1_hbm.1, bf16[64,256]{1,0:T(8,128)(2,1)} %z2_hbm.1, bf16[10,64,256]{2,1,0:T(8,128)(2,1)} %zs_hbm.1, bf16[8192,256]{1,0:T(8,128)(2,1)} %c_hbm.1), custom_call_target="tpu_custom_call" | custom-call | tf_op jit(solution)/shard_map/swav_step/pallas_call | solution.py:456
  61.3 5.4 %write_out.1 = (f32[64,8192]{1,0:T(8,128)}, f32[64,8192]{1,0:T(8,128)}, f32[1,1]{1,0:T(1,128)}, f32[64,256]{1,0:T(8,128)}, f32[64,256]{1,0:T(8,128)}, /*index=5*/f32[10,64,256]{2,1,0:T(8,128)}, f32[8192,256]{1,0:T(8,128)}) custom-call(f32[2,64,8192]{2,1,0:T(8,128)S(1)} %get-tuple-element.18.q_ref, f32[1,128]{1,0:T(1,128)S(1)} %get-tuple-element.19.loss_in, ...), custom_call_target="tpu_custom_call" | custom-call | tf_op jit(solution)/shard_map/write_out/pallas_call | solution.py:499

commit v12 on v10

--- a/solution.py
+++ b/solution.py
@@ -339,14 +339,6 @@
             acopy(dev, ch, partner, 3 + kind).start()
 
     bcast(*v_args, wait=True)
-    for view in range(2):
-        for blk in range(OWN // 128):
-            lanes = slice(blk * 128, (blk + 1) * 128)
-            vb[view, lanes] = jnp.broadcast_to(vx[dg, view, :, lanes], (128, 128)).T
-    exp_views(0, VIEWS, dg * OWN)
-    lax.fori_loop(0, NCH, dc_far, 0)
-    forward(0)
-    forward(1)
 
     lanes = pl.ds(pl.multiple_of((me // 2) * 128, 128), 128)
     for view in range(VIEWS):
@@ -397,14 +389,23 @@
         dz_out[...] += dz.reshape(VIEWS, ROWS, DIM)
         return acc + fold(dot)
     acc = lax.fori_loop(0, PROTOS // PC - KEPT, row_chunk, jnp.zeros((8, PC), F32))
-    forward(2)
     row_kept = functools.partial(row_chunk, kept=True)
-    acc = lax.fori_loop(PROTOS // PC - KEPT, PROTOS // PC - 2, row_kept, acc)
-    forward(3)
-    acc = lax.fori_loop(PROTOS // PC - 2, PROTOS // PC, row_kept, acc)
+    acc = lax.fori_loop(PROTOS // PC - KEPT, PROTOS // PC, row_kept, acc)
     cross = jnp.sum(jnp.sum(acc, axis=0, keepdims=True), axis=1, keepdims=True)
     px[me] = jnp.broadcast_to(cross, (1, 128))
     bcast(*p_args, wait=False)
+    forward(0)
+    for view in range(2):
+        for blk in range(OWN // 128):
+            lanes = slice(blk * 128, (blk + 1) * 128)
+            vb[view, lanes] = jnp.broadcast_to(vx[dg, view, :, lanes], (128, 128)).T
+    exp_views(0, VIEWS, dg * OWN)
+    forward(1)
+    lax.fori_loop(0, 2, dc_far, 0)
+    forward(2)
+    lax.fori_loop(2, NCH, dc_far, 0)
+    forward(3)
+
 
     bcast(*p_args, wait=True)
     tot = px[0]

time: 65.7 us -> 64 us (0.974)
  Pallas kernels: 65 us -> 63.3 us
    pallas_call x1, Pallas kernels: 59.6 us -> 57.9 us  [local_step(): pl.pallas_call(body, out_shape=(pltpu.VMEM((2, ROWS, PROTOS), F32), pltpu...]
where the time goes in v12:
time: 64 us; the launch traced here: 63.9 us
  Pallas kernels  63.3 us (99%)
  between operations  0.64 us (1%)
    pallas_call x1, Pallas kernels, local_step(): pl.pallas_call(body, out_shape=(pltpu.VMEM((2, ROWS, PROTOS), F32), pltpu...  57.9 us
    pallas_call x1, Pallas kernels, local_step(): pl.pallas_call(write_out, out_shape=(jax.ShapeDtypeStruct((ROWS, PROTOS),...  5.43 us

profile of v12, /device:TPU:0, one launch (start us, length us, event | category | flops | bytes accessed | tf_op | source)
XLA Modules:
  0.0 63.9 jit_solution(14902609026948415988)
XLA Ops:
  0.6 57.9 %swav_step.1 = (f32[2,64,8192]{2,1,0:T(8,128)S(1)}, f32[1,128]{1,0:T(1,128)S(1)}, f32[12,64,256]{2,1,0:T(8,128)S(1)}, f32[8192,256]{1,0:T(8,128)S(1)}) custom-call(s32[1,64]{1,0:T(1,128)} %bitcast.2, bf16[64,256]{1,0:T(8,128)(2,1)} %z1_hbm.1, bf16[64,256]{1,0:T(8,128)(2,1)} %z2_hbm.1, bf16[10,64,256]{2,1,0:T(8,128)(2,1)} %zs_hbm.1, bf16[8192,256]{1,0:T(8,128)(2,1)} %c_hbm.1), custom_call_target="tpu_custom_call" | custom-call | tf_op jit(solution)/shard_map/swav_step/pallas_call | solution.py:459
  58.5 5.4 %write_out.1 = (f32[64,8192]{1,0:T(8,128)}, f32[64,8192]{1,0:T(8,128)}, f32[1,1]{1,0:T(1,128)}, f32[64,256]{1,0:T(8,128)}, f32[64,256]{1,0:T(8,128)}, /*index=5*/f32[10,64,256]{2,1,0:T(8,128)}, f32[8192,256]{1,0:T(8,128)}) custom-call(f32[2,64,8192]{2,1,0:T(8,128)S(1)} %get-tuple-element.18.q_ref, f32[1,128]{1,0:T(1,128)S(1)} %get-tuple-element.19.loss_in, ...), custom_call_target="tpu_custom_call" | custom-call | tf_op jit(solution)/shard_map/write_out/pallas_call | solution.py:501

commit v13 on v12

--- a/solution.py
+++ b/solution.py
@@ -20,7 +20,7 @@
 OWN = PROTOS // DEVS
 KC = 256
 NCH = OWN // KC
-KEPT = 8
+KEPT = 10
 PC = 512
 MESH = pl.DeviceIdType.MESH
 F32 = jnp.float32
@@ -219,7 +219,7 @@
 
     lax.fori_loop(0, 6, sum_chunk, 0)
     zforward((0, 1))
-    lax.fori_loop(6, 8, sum_chunk, 0)
+    lax.fori_loop(6, 8, functools.partial(sum_chunk, keep=True), 0)
     bcast(*m_args, wait=True)
     zfinish((0, 1))
     for q in range(NROW // 128):
@@ -262,7 +262,7 @@
 
     sink_pass(0)
     zstart(3)
-    lax.fori_loop(PROTOS // PC - KEPT, PROTOS // PC, functools.partial(sum_chunk, keep=True), 0)
+    lax.fori_loop(8, PROTOS // PC, functools.partial(sum_chunk, keep=True), 0)
     zforward((2,))
     sink_close(0)
     sink_pass(1)
@@ -495,7 +495,7 @@
             dma((6, NCH)), dma((6, NCH)),
         ],
         compiler_params=pltpu.CompilerParams(
-            collective_id=0, has_side_effects=True, vmem_limit_bytes=50 * 1024 * 1024),
+            collective_id=0, has_side_effects=True, vmem_limit_bytes=51 * 1024 * 1024),
         name="swav_step",
     )(live_mask.reshape(1, ROWS), z_one, z_two, z_small, protos)
     q_one, q_two, loss, dz_one, dz_two, dz_small, d_protos = pl.pallas_call(

time: 64 us -> 63.8 us (level)
  no operation moved by 1% of the time
where the time goes in v13:
time: 63.8 us; the launch traced here: 63.7 us
  Pallas kernels  63 us (99%)
  between operations  0.64 us (1%)
    pallas_call x1, Pallas kernels, local_step(): pl.pallas_call(body, out_shape=(pltpu.VMEM((2, ROWS, PROTOS), F32), pltpu...  57.6 us
    pallas_call x1, Pallas kernels, local_step(): pl.pallas_call(write_out, out_shape=(jax.ShapeDtypeStruct((ROWS, PROTOS),...  5.43 us

profile of v13, /device:TPU:0, one launch (start us, length us, event | category | flops | bytes accessed | tf_op | source)
XLA Modules:
  0.0 63.7 jit_solution(12861356334089407920)
XLA Ops:
  0.6 57.6 %swav_step.1 = (f32[2,64,8192]{2,1,0:T(8,128)S(1)}, f32[1,128]{1,0:T(1,128)S(1)}, f32[12,64,256]{2,1,0:T(8,128)S(1)}, f32[8192,256]{1,0:T(8,128)S(1)}) custom-call(s32[1,64]{1,0:T(1,128)} %bitcast.2, bf16[64,256]{1,0:T(8,128)(2,1)} %z1_hbm.1, bf16[64,256]{1,0:T(8,128)(2,1)} %z2_hbm.1, bf16[10,64,256]{2,1,0:T(8,128)(2,1)} %zs_hbm.1, bf16[8192,256]{1,0:T(8,128)(2,1)} %c_hbm.1), custom_call_target="tpu_custom_call" | custom-call | tf_op jit(solution)/shard_map/swav_step/pallas_call | solution.py:459
  58.2 5.4 %write_out.1 = (f32[64,8192]{1,0:T(8,128)}, f32[64,8192]{1,0:T(8,128)}, f32[1,1]{1,0:T(1,128)}, f32[64,256]{1,0:T(8,128)}, f32[64,256]{1,0:T(8,128)}, /*index=5*/f32[10,64,256]{2,1,0:T(8,128)}, f32[8192,256]{1,0:T(8,128)}) custom-call(f32[2,64,8192]{2,1,0:T(8,128)S(1)} %get-tuple-element.18.q_ref, f32[1,128]{1,0:T(1,128)S(1)} %get-tuple-element.19.loss_in, ...), custom_call_target="tpu_custom_call" | custom-call | tf_op jit(solution)/shard_map/write_out/pallas_call | solution.py:501
